TPU v7x, 512 devices: a whole 4x8x8 slice. The times are simulated.
512 devices in a mesh: tm: 32 (over x_hi, y, core), space: 16 (over x_lo, z).
Axes of the slice: x: 4 (x_hi: 2, x_lo: 2; x = x_hi * 2 + x_lo), y: 8, z: 8, core: 2. Of those that a mesh axis runs over, the one named last changes fastest.
Arguments:
- increments: float32 [64, 1024, 2048], P('tm', 'space'), may hold values from -6 to 6
- precision: float32 [64, 1024, 2048], P('tm', 'space'), may hold values from 0.5 to 4
- courant_rows: float32 [1024, 2048], P('space'), may hold values from 0.05 to 0.45
- courant_cols: float32 [1024, 2048], P('space'), may hold values from 0.05 to 0.45
- wind_codes: int32 [64, 128, 16], P('tm', 'space'), may hold values from 0 to 3
Outputs:
- misfit: float32 [64, 1024, 2048], P('tm', 'space')
- adjoint_image: float32 [64, 1024, 2048], P('tm', 'space')
All inputs are finite; a program needn't handle non-finite values.
Results may differ from a plain program's by a relative error of at most 0.00002.
Values sent between devices are 32-bit elements; how exact they have to be, the bound alone decides.
No kernel may reach another device: no remote copies, remote signals or barrier semaphores. Data moves between devices by JAX's collectives and lax.ppermute only.
A program may use at most 64 MiB of HBM per device.

v0:
```python
import jax
import jax.numpy as jnp
from jax import lax
from jax.sharding import PartitionSpec as P

BX = 8
BY = 128
SWEEPS = 2


def padded_2(block, sides, width):
    for axis, dim in sides:
        count = lax.axis_size(axis)
        forward = [(i, i + 1) for i in range(count - 1)]
        backward = [(target, source) for source, target in forward]
        low = lax.ppermute(
            lax.slice_in_dim(block, block.shape[dim] - width, None, axis=dim), axis, forward
        )
        high = lax.ppermute(lax.slice_in_dim(block, 0, width, axis=dim), axis, backward)
        block = jnp.concatenate([low, block, high], axis=dim)
    return block


def passed_along(value, axis, steps):
    count = lax.axis_size(axis)
    first, last = (max(0, -steps), min(count, count - steps))
    return lax.ppermute(value, axis, [(source, source + steps) for source in range(first, last)])


def directions(wind_codes):
    per_cell = jnp.repeat(jnp.repeat(wind_codes, BX, axis=1), BY, axis=2)
    side_rows = 1 - 2 * (per_cell % 2)
    side_cols = 1 - 2 * (per_cell // 2)
    return (side_rows, side_cols)


def advance(values_in, side_rows, side_cols, courant_rows, courant_cols):
    padded = padded_2(values_in, (("space", 1),), 1)
    from_rows = jnp.where(side_rows > 0, padded[:, :-2], padded[:, 2:])
    from_cols = jnp.where(
        side_cols > 0, jnp.roll(values_in, 1, axis=2), jnp.roll(values_in, -1, axis=2)
    )
    return (
        (1.0 - courant_rows - courant_cols) * values_in
        + courant_rows * from_rows
        + courant_cols * from_cols
    )


def smooth(values_in):
    slab_rows = values_in.shape[1]
    total_rows = slab_rows * lax.axis_size("space")
    first_row = lax.axis_index("space") * slab_rows
    field = padded_2(values_in, (("space", 1),), SWEEPS)
    for sweep in range(SWEEPS):
        margin = SWEEPS - 1 - sweep
        middle = field[:, 1:-1]
        beside_all = (
            field[:, :-2]
            + field[:, 2:]
            + jnp.roll(middle, 1, axis=2)
            + jnp.roll(middle, -1, axis=2)
        )
        updated = middle + 0.2 * (beside_all - 4.0 * middle)
        global_rows = first_row - margin + jnp.arange(updated.shape[1], dtype=jnp.int32)
        inside = (global_rows >= 0) & (global_rows < total_rows)
        field = jnp.where(inside[None, :, None], updated, 0.0)
    return field


def retreat(values_in, side_rows, side_cols, courant_rows, courant_cols):
    along_rows = courant_rows * values_in
    pieces = jnp.stack(
        [jnp.where(side_rows > 0, along_rows, 0.0), jnp.where(side_rows < 0, along_rows, 0.0)],
        axis=1,
    )
    downward = pieces[:, 0]
    upward = pieces[:, 1]
    from_above = passed_along(downward[:, :1], "space", -1)
    from_below = passed_along(upward[:, -1:], "space", 1)
    from_rows = jnp.concatenate([downward[:, 1:], from_above], axis=1) + jnp.concatenate(
        [from_below, upward[:, :-1]], axis=1
    )
    along_cols = courant_cols * values_in
    plus_cols = jnp.where(side_cols > 0, along_cols, 0.0)
    minus_cols = jnp.where(side_cols < 0, along_cols, 0.0)
    from_cols = jnp.roll(plus_cols, -1, axis=2) + jnp.roll(minus_cols, 1, axis=2)
    return (1.0 - courant_rows - courant_cols) * values_in + from_rows + from_cols


def on_device(increments, precision, courant_rows, courant_cols, wind_codes):
    incoming = passed_along(increments[1], "tm", 1)
    side_rows, side_cols = directions(wind_codes)
    inputs = jnp.stack([incoming, increments[0]])
    moved = advance(inputs, side_rows, side_cols, courant_rows, courant_cols)
    misfit = increments - moved
    weighted = smooth(precision * smooth(misfit))
    images = retreat(weighted, side_rows, side_cols, courant_rows, courant_cols)
    from_next = passed_along(images[0], "tm", -1)
    adjoint_image = jnp.stack([weighted[0] - images[1], weighted[1] - from_next])
    return (misfit, adjoint_image)


def solution(mesh):
    in_specs = (
        P("tm", "space", None),
        P("tm", "space", None),
        P("space", None),
        P("space", None),
        P("tm", "space", None),
    )
    out_specs = (P("tm", "space", None), P("tm", "space", None))
    return jax.shard_map(
        on_device, mesh=mesh, in_specs=in_specs, out_specs=out_specs, check_vma=False
    )
```

profile of v0, /device:TPU:59, one launch (start us, length us, event | category | flops | bytes accessed | tf_op | source)
XLA Modules:
  0.0 87.9 jit_solution(13781868956556519771)
XLA Ops:
  0.6 0.0 copy-start
  0.6 2.1 %slice_bitcast_fusion.2 = (f32[64,2048]{1,0:T(8,128)}, f32[1,64,2048]{2,1,0:T(8,128)S(1)}) fusion(f32[2,64,2048]{2,1,0:T(8,128)} %param.5), kind=kLoop, calls=%fused_computation.98 | loop fusion | bytes 2097152 | tf_op jit(solution)/shard_map/squeeze | solution.py:92
  2.7 3.5 %collective-permute-start = (f32[64,2048]{1,0:T(8,128)}, f32[64,2048]{1,0:T(8,128)S(1)}, u32[]{:S(2)}, u32[]{:S(2)}) collective-permute-start(f32[64,2048]{1,0:T(8,128)} %get-tuple-element.31), channel_id=1, source_target_pairs={{0,16},{16,32},{32,48},{48,64},{64,80},{80,96},{96,112},{112,128},... | collective-permute-start | bytes 1572872 | tf_op jit(solution)/shard_map/ppermute | solution.py:27
  6.3 1.3 %broadcast_in_dim.54 = s32[2,64,16,128]{3,2,1,0:T(8,128)} broadcast(s32[2,64,16]{2,1,0:T(8,128)S(1)} %broadcast_bitcast_fusion), dimensions={0,1,2} | broadcast | bytes 1056768 | tf_op jit(solution)/shard_map/broadcast_in_dim | solution.py:31
  7.6 1.5 %reshape.28 = s32[2,64,2048]{2,1,0:T(8,128)S(1)} reshape(s32[2,64,16,128]{3,2,1,0:T(8,128)} %broadcast_in_dim.54) | data formatting | bytes 2097152 | tf_op jit(solution)/shard_map/reshape | solution.py:31
  9.1 0.0 copy-done.3
  9.1 0.1 subtract_subtract_fusion
  9.2 3.5 %collective-permute-done = f32[64,2048]{1,0:T(8,128)S(1)} collective-permute-done((f32[64,2048]{1,0:T(8,128)}, f32[64,2048]{1,0:T(8,128)S(1)}, u32[]{:S(2)}, u32[]{:S(2)}) %collective-permute-start) | collective-permute-done | bytes 524320 | tf_op jit(solution)/shard_map/ppermute | solution.py:27
  12.7 0.4 fusion.21
  13.0 0.0 copy-start.4
  13.0 4.1 %collective-permute-start.1 = (f32[2,1,2048]{2,1,0:T(1,128)S(1)}, f32[2,1,2048]{2,1,0:T(1,128)S(1)}, u32[]{:S(2)}, u32[]{:S(2)}) collective-permute-start(f32[2,1,2048]{2,1,0:T(1,128)S(1)} %get-tuple-element.29), channel_id=1, source_target_pairs={{0,1},{1,2},{2,3},{3,4},{4,5},{5,6},{6,7},{7,8},{8,9},{9,10},{10,1... | collective-permute-start | bytes 49160 | tf_op jit(solution)/shard_map/ppermute | solution.py:16
  17.2 9.5 %collective-permute-start.2 = (f32[2,1,2048]{2,1,0:T(1,128)S(1)}, f32[2,1,2048]{2,1,0:T(1,128)S(1)}, u32[]{:S(2)}, u32[]{:S(2)}) collective-permute-start(f32[2,1,2048]{2,1,0:T(1,128)S(1)} %get-tuple-element.30), channel_id=1, source_target_pairs={{1,0},{2,1},{3,2},{4,3},{5,4},{6,5},{7,6},{8,7},{9,8},{10,9},{11,1... | collective-permute-start | bytes 49160 | tf_op jit(solution)/shard_map/ppermute | solution.py:19
  26.7 0.1 fusion.49
  26.7 0.8 collective-permute-done.2
  27.5 1.9 %fusion.25 = f32[2,64,2048]{2,1,0:T(8,128)S(1)} fusion(f32[2,64,2048]{2,1,0:T(8,128)S(1)} %copy-done.4, f32[1,64,2048]{2,1,0:T(8,128)S(1)} %get-tuple-element.32, f32[1,64,2048]{2,1,0:T(8,128)S(1)} %bitcast.22, f32[2,1,2048]{2,1,0:T(1,128)S(1)} %collective-permute-done.2, f32[2,1,2048]{2,1,0:T(1,128)S(1)} %collective-permute-done.1, ...), kind=kLoop, calls=%fused_computation.55 | loop fusion | flops 10485760 | bytes 7897088 | tf_op jit(solution)/shard_map/sub | solution.py:96
  29.5 0.0 copy-start.1
  29.5 1.9 %collective-permute-start.3 = (f32[2,2,2048]{2,1,0:T(2,128)S(1)}, f32[2,2,2048]{2,1,0:T(2,128)S(1)}, u32[]{:S(2)}, u32[]{:S(2)}) collective-permute-start(f32[2,2,2048]{2,1,0:T(2,128)S(1)} %get-tuple-element.23), channel_id=1, source_target_pairs={{0,1},{1,2},{2,3},{3,4},{4,5},{5,6},{6,7},{7,8},{8,9},{9,10},{10,1... | collective-permute-start | bytes 98312 | tf_op jit(solution)/shard_map/ppermute | solution.py:16
  31.4 5.7 %collective-permute-start.4 = (f32[2,2,2048]{2,1,0:T(2,128)S(1)}, f32[2,2,2048]{2,1,0:T(2,128)S(1)}, u32[]{:S(2)}, u32[]{:S(2)}) collective-permute-start(f32[2,2,2048]{2,1,0:T(2,128)S(1)} %get-tuple-element.24), channel_id=1, source_target_pairs={{1,0},{2,1},{3,2},{4,3},{5,4},{6,5},{7,6},{8,7},{9,8},{10,9},{11,1... | collective-permute-start | bytes 98312 | tf_op jit(solution)/shard_map/ppermute | solution.py:19
  37.2 1.0 %collective-permute-done.4 = f32[2,2,2048]{2,1,0:T(2,128)S(1)} collective-permute-done((f32[2,2,2048]{2,1,0:T(2,128)S(1)}, f32[2,2,2048]{2,1,0:T(2,128)S(1)}, u32[]{:S(2)}, u32[]{:S(2)}) %collective-permute-start.4) | collective-permute-done | bytes 32800 | tf_op jit(solution)/shard_map/ppermute | solution.py:19
  38.2 0.2 pad_maximum_fusion.9
  38.4 0.4 fusion.58
  38.8 0.7 fusion.13
  39.5 0.1 fusion.57
  39.6 0.4 fusion.56
  40.0 0.8 copy-done.5
  40.9 0.6 fusion.38
  41.5 1.9 %collective-permute-start.5 = (f32[2,2,2048]{2,1,0:T(2,128)S(1)}, f32[2,2,2048]{2,1,0:T(2,128)S(1)}, u32[]{:S(2)}, u32[]{:S(2)}) collective-permute-start(f32[2,2,2048]{2,1,0:T(2,128)S(1)} %get-tuple-element.21), channel_id=1, source_target_pairs={{0,1},{1,2},{2,3},{3,4},{4,5},{5,6},{6,7},{7,8},{8,9},{9,10},{10,1... | collective-permute-start | bytes 98312 | tf_op jit(solution)/shard_map/ppermute | solution.py:16
  43.4 5.8 %collective-permute-start.6 = (f32[2,2,2048]{2,1,0:T(2,128)S(1)}, f32[2,2,2048]{2,1,0:T(2,128)S(1)}, u32[]{:S(2)}, u32[]{:S(2)}) collective-permute-start(f32[2,2,2048]{2,1,0:T(2,128)S(1)} %get-tuple-element.22), channel_id=1, source_target_pairs={{1,0},{2,1},{3,2},{4,3},{5,4},{6,5},{7,6},{8,7},{9,8},{10,9},{11,1... | collective-permute-start | bytes 98312 | tf_op jit(solution)/shard_map/ppermute | solution.py:19
  49.2 1.0 %collective-permute-done.6 = f32[2,2,2048]{2,1,0:T(2,128)S(1)} collective-permute-done((f32[2,2,2048]{2,1,0:T(2,128)S(1)}, f32[2,2,2048]{2,1,0:T(2,128)S(1)}, u32[]{:S(2)}, u32[]{:S(2)}) %collective-permute-start.6) | collective-permute-done | bytes 32800 | tf_op jit(solution)/shard_map/ppermute | solution.py:19
  50.2 0.1 pad_maximum_fusion.10
  50.4 0.4 fusion.55
  50.8 0.7 fusion.5
  51.5 0.1 fusion.53
  51.6 0.4 fusion.54
  52.0 1.2 %compare_select_fusion = (f32[2,64,2048]{2,1,0:T(8,128)S(1)}, f32[2,64,2048]{2,1,0:T(8,128)S(1)}) fusion(f32[64,2048]{1,0:T(8,128)S(1)} %copy-done.2, s32[2,64,2048]{2,1,0:T(8,128)S(1)} %reshape.28, f32[2,64,1]{2,1,0:T(8,128)S(1)} %get-tuple-element.8, f32[2,64,2047]{2,1,0:T(8,128)S(1)} %get-tuple-element.10, f32[2,64,2047]{2,1,0:T(8,128)S(1)} %get-tuple-element.9, ...), kind=kLoop, calls=%fused_computation.86 | loop fusion | flops 7864320 | bytes 8912960 | tf_op jit(solution)/shard_map/jit(_where)/select_n | solution.py:86
  53.2 1.3 %compare_select_fusion.1 = (f32[2,64,2048]{2,1,0:T(8,128)S(1)}, f32[2,64,2048]{2,1,0:T(8,128)S(1)}, f32[2,64,2048]{2,1,0:T(8,128)S(1)}) fusion(f32[2,64,2048]{2,1,0:T(8,128)S(1)} %get-tuple-element.3, f32[64,2048]{1,0:T(8,128)S(1)} %copy-done.3, s32[2,64,2048]{2,1,0:T(8,128)S(1)} %reshape.28, f32[64,2048]{1,0:T(8,128)S(1)} %copy-done.2), kind=kLoop, calls=%fused_computation.87 | loop fusion | flops 8126464 | bytes 6291456 | tf_op jit(solution)/shard_map/jit(_where)/select_n | solution.py:74
  54.6 5.8 %collective-permute-start.7 = (f32[2,1,2048]{2,1,0:T(1,128)S(1)}, f32[2,1,2048]{2,1,0:T(1,128)S(1)}, u32[]{:S(2)}, u32[]{:S(2)}) collective-permute-start(f32[2,1,2048]{2,1,0:T(1,128)S(1)} %slice.272), channel_id=1, source_target_pairs={{1,0},{2,1},{3,2},{4,3},{5,4},{6,5},{7,6},{8,7},{9,8},{10,9},{11,1... | collective-permute-start | bytes 49160 | tf_op jit(solution)/shard_map/ppermute | solution.py:27
  60.3 1.9 %collective-permute-start.8 = (f32[2,1,2048]{2,1,0:T(1,128)S(1)}, f32[2,1,2048]{2,1,0:T(1,128)S(1)}, u32[]{:S(2)}, u32[]{:S(2)}) collective-permute-start(f32[2,1,2048]{2,1,0:T(1,128)S(1)} %slice.273), channel_id=1, source_target_pairs={{0,1},{1,2},{2,3},{3,4},{4,5},{5,6},{6,7},{7,8},{8,9},{9,10},{10,1... | collective-permute-start | bytes 49160 | tf_op jit(solution)/shard_map/ppermute | solution.py:27
  62.3 0.1 slice.271
  62.4 0.3 slice.275
  62.7 0.1 slice.277
  62.8 4.1 %collective-permute-done.8 = f32[2,1,2048]{2,1,0:T(1,128)S(1)} collective-permute-done((f32[2,1,2048]{2,1,0:T(1,128)S(1)}, f32[2,1,2048]{2,1,0:T(1,128)S(1)}, u32[]{:S(2)}, u32[]{:S(2)}) %collective-permute-start.8) | collective-permute-done | bytes 16416 | tf_op jit(solution)/shard_map/ppermute | solution.py:27
  66.9 0.7 fusion.43
  67.6 0.1 slice_subtract_fusion
  67.7 7.3 %collective-permute-start.9 = (f32[64,2048]{1,0:T(8,128)S(1)}, f32[64,2048]{1,0:T(8,128)S(1)}, u32[]{:S(2)}, u32[]{:S(2)}) collective-permute-start(f32[64,2048]{1,0:T(8,128)S(1)} %get-tuple-element.20), channel_id=1, source_target_pairs={{16,0},{32,16},{48,32},{64,48},{80,64},{96,80},{112,96},{128,112},... | collective-permute-start | bytes 1572872 | tf_op jit(solution)/shard_map/ppermute | solution.py:27
  75.1 11.7 %collective-permute-done.9 = f32[64,2048]{1,0:T(8,128)S(1)} collective-permute-done((f32[64,2048]{1,0:T(8,128)S(1)}, f32[64,2048]{1,0:T(8,128)S(1)}, u32[]{:S(2)}, u32[]{:S(2)}) %collective-permute-start.9) | collective-permute-done | bytes 524320 | tf_op jit(solution)/shard_map/ppermute | solution.py:27
  86.8 0.1 fusion.47
  86.8 1.0 %pad_maximum_fusion.15 = f32[2,64,2048]{2,1,0:T(8,128)} fusion(f32[1,64,2048]{2,1,0:T(8,128)S(1)} %fusion.47, f32[1,64,2048]{2,1,0:T(8,128)S(1)} %get-tuple-element.19), kind=kLoop, calls=%fused_computation.83 | loop fusion | flops 262144 | bytes 2097152 | tf_op jit(solution)/shard_map/stack | solution.py:100
  (20 shorter events, 0.2 us)
Async XLA Ops:
  0.6 5.6 %copy-start = (s32[2,8,16]{2,1,0:T(8,128)S(1)}, s32[2,8,16]{2,1,0:T(8,128)}, u32[]{:S(2)}) copy-start(s32[2,8,16]{2,1,0:T(8,128)} %param.9) | copy-start | bytes 3076
  2.7 9.9 %collective-permute-start = (f32[64,2048]{1,0:T(8,128)}, f32[64,2048]{1,0:T(8,128)S(1)}, u32[]{:S(2)}, u32[]{:S(2)}) collective-permute-start(f32[64,2048]{1,0:T(8,128)} %get-tuple-element.31), channel_id=1, source_target_pairs={{0,16},{16,32},{32,48},{48,64},{64,80},{80,96},{96,112},{112,128},... | collective-permute-start | bytes 1572872 | tf_op jit(solution)/shard_map/ppermute | solution.py:27
  7.6 1.5 %copy-start.2 = (f32[64,2048]{1,0:T(8,128)S(1)}, f32[64,2048]{1,0:T(8,128)}, u32[]{:S(2)}) copy-start(f32[64,2048]{1,0:T(8,128)} %param.8) | copy-start | bytes 1572868
  7.6 1.5 %copy-start.3 = (f32[64,2048]{1,0:T(8,128)S(1)}, f32[64,2048]{1,0:T(8,128)}, u32[]{:S(2)}) copy-start(f32[64,2048]{1,0:T(8,128)} %param.7) | copy-start | bytes 1572868
  13.0 14.5 %copy-start.4 = (f32[2,64,2048]{2,1,0:T(8,128)S(1)}, f32[2,64,2048]{2,1,0:T(8,128)}, u32[]{:S(2)}) copy-start(f32[2,64,2048]{2,1,0:T(8,128)} %param.5) | copy-start | bytes 3145732
  13.0 13.7 %collective-permute-start.1 = (f32[2,1,2048]{2,1,0:T(1,128)S(1)}, f32[2,1,2048]{2,1,0:T(1,128)S(1)}, u32[]{:S(2)}, u32[]{:S(2)}) collective-permute-start(f32[2,1,2048]{2,1,0:T(1,128)S(1)} %get-tuple-element.29), channel_id=1, source_target_pairs={{0,1},{1,2},{2,3},{3,4},{4,5},{5,6},{6,7},{7,8},{8,9},{9,10},{10,1... | collective-permute-start | bytes 49160 | tf_op jit(solution)/shard_map/ppermute | solution.py:16
  17.2 10.3 %collective-permute-start.2 = (f32[2,1,2048]{2,1,0:T(1,128)S(1)}, f32[2,1,2048]{2,1,0:T(1,128)S(1)}, u32[]{:S(2)}, u32[]{:S(2)}) collective-permute-start(f32[2,1,2048]{2,1,0:T(1,128)S(1)} %get-tuple-element.30), channel_id=1, source_target_pairs={{1,0},{2,1},{3,2},{4,3},{5,4},{6,5},{7,6},{8,7},{9,8},{10,9},{11,1... | collective-permute-start | bytes 49160 | tf_op jit(solution)/shard_map/ppermute | solution.py:19
  29.5 9.3 %copy-start.1 = (f32[2,64,2048]{2,1,0:T(8,128)}, f32[2,64,2048]{2,1,0:T(8,128)S(1)}, u32[]{:S(2)}) copy-start(f32[2,64,2048]{2,1,0:T(8,128)S(1)} %fusion.25) | copy-start | bytes 3145732
  29.5 7.7 %collective-permute-start.3 = (f32[2,2,2048]{2,1,0:T(2,128)S(1)}, f32[2,2,2048]{2,1,0:T(2,128)S(1)}, u32[]{:S(2)}, u32[]{:S(2)}) collective-permute-start(f32[2,2,2048]{2,1,0:T(2,128)S(1)} %get-tuple-element.23), channel_id=1, source_target_pairs={{0,1},{1,2},{2,3},{3,4},{4,5},{5,6},{6,7},{7,8},{8,9},{9,10},{10,1... | collective-permute-start | bytes 98312 | tf_op jit(solution)/shard_map/ppermute | solution.py:16
  31.4 6.7 %collective-permute-start.4 = (f32[2,2,2048]{2,1,0:T(2,128)S(1)}, f32[2,2,2048]{2,1,0:T(2,128)S(1)}, u32[]{:S(2)}, u32[]{:S(2)}) collective-permute-start(f32[2,2,2048]{2,1,0:T(2,128)S(1)} %get-tuple-element.24), channel_id=1, source_target_pairs={{1,0},{2,1},{3,2},{4,3},{5,4},{6,5},{7,6},{8,7},{9,8},{10,9},{11,1... | collective-permute-start | bytes 98312 | tf_op jit(solution)/shard_map/ppermute | solution.py:19
  39.6 1.2 %copy-start.5 = (f32[2,64,2048]{2,1,0:T(8,128)S(1)}, f32[2,64,2048]{2,1,0:T(8,128)}, u32[]{:S(2)}) copy-start(f32[2,64,2048]{2,1,0:T(8,128)} %param.6) | copy-start | bytes 3145732
  41.5 7.7 %collective-permute-start.5 = (f32[2,2,2048]{2,1,0:T(2,128)S(1)}, f32[2,2,2048]{2,1,0:T(2,128)S(1)}, u32[]{:S(2)}, u32[]{:S(2)}) collective-permute-start(f32[2,2,2048]{2,1,0:T(2,128)S(1)} %get-tuple-element.21), channel_id=1, source_target_pairs={{0,1},{1,2},{2,3},{3,4},{4,5},{5,6},{6,7},{7,8},{8,9},{9,10},{10,1... | collective-permute-start | bytes 98312 | tf_op jit(solution)/shard_map/ppermute | solution.py:16
  43.4 6.8 %collective-permute-start.6 = (f32[2,2,2048]{2,1,0:T(2,128)S(1)}, f32[2,2,2048]{2,1,0:T(2,128)S(1)}, u32[]{:S(2)}, u32[]{:S(2)}) collective-permute-start(f32[2,2,2048]{2,1,0:T(2,128)S(1)} %get-tuple-element.22), channel_id=1, source_target_pairs={{1,0},{2,1},{3,2},{4,3},{5,4},{6,5},{7,6},{8,7},{9,8},{10,9},{11,1... | collective-permute-start | bytes 98312 | tf_op jit(solution)/shard_map/ppermute | solution.py:19
  54.6 8.2 %collective-permute-start.7 = (f32[2,1,2048]{2,1,0:T(1,128)S(1)}, f32[2,1,2048]{2,1,0:T(1,128)S(1)}, u32[]{:S(2)}, u32[]{:S(2)}) collective-permute-start(f32[2,1,2048]{2,1,0:T(1,128)S(1)} %slice.272), channel_id=1, source_target_pairs={{1,0},{2,1},{3,2},{4,3},{5,4},{6,5},{7,6},{8,7},{9,8},{10,9},{11,1... | collective-permute-start | bytes 49160 | tf_op jit(solution)/shard_map/ppermute | solution.py:27
  60.3 6.6 %collective-permute-start.8 = (f32[2,1,2048]{2,1,0:T(1,128)S(1)}, f32[2,1,2048]{2,1,0:T(1,128)S(1)}, u32[]{:S(2)}, u32[]{:S(2)}) collective-permute-start(f32[2,1,2048]{2,1,0:T(1,128)S(1)} %slice.273), channel_id=1, source_target_pairs={{0,1},{1,2},{2,3},{3,4},{4,5},{5,6},{6,7},{7,8},{8,9},{9,10},{10,1... | collective-permute-start | bytes 49160 | tf_op jit(solution)/shard_map/ppermute | solution.py:27
  67.7 19.0 %collective-permute-start.9 = (f32[64,2048]{1,0:T(8,128)S(1)}, f32[64,2048]{1,0:T(8,128)S(1)}, u32[]{:S(2)}, u32[]{:S(2)}) collective-permute-start(f32[64,2048]{1,0:T(8,128)S(1)} %get-tuple-element.20), channel_id=1, source_target_pairs={{16,0},{32,16},{48,32},{64,48},{80,64},{96,80},{112,96},{128,112},... | collective-permute-start | bytes 1572872 | tf_op jit(solution)/shard_map/ppermute | solution.py:27
where the time goes:
time: 88.3 us; the launch traced here: 87.9 us
  starting transfers between devices  47.4 us (54%)
  waiting for transfers between devices  22 us (25%)
  other arithmetic  9.29 us (11%)
  local copies, waits for them, and re-layouts  8.12 us (9%)
  between operations  0.98 us (1%)
    ppermute x3, starting transfers between devices, padded_2(): lax.ppermute(lax.slice_in_dim(block, 0, width, axis=dim), axis, backward)  21 us
    ppermute x4, waiting for transfers between devices, passed_along(): lax.ppermute(value, axis, [(source, source + steps) for source in range(f...  19.3 us
    ppermute x4, starting transfers between devices, passed_along(): lax.ppermute(value, axis, [(source, source + steps) for source in range(f...  18.5 us
    ppermute x3, starting transfers between devices, padded_2(): lax.ppermute(lax.slice_in_dim(block, block.shape[dim] - width, None, axis...  7.97 us
    ppermute x3, waiting for transfers between devices, padded_2(): lax.ppermute(lax.slice_in_dim(block, 0, width, axis=dim), axis, backward)  2.73 us
    squeeze x1, local copies, waits for them, and re-layouts, on_device(): incoming = passed_along(increments[1], 'tm', 1)  2.07 us
    sub x1, other arithmetic, on_device(): misfit = increments - moved  1.95 us
  transfers between devices with their start and end apart: 10, of which 6 were waited for; matrix products, arithmetic and copies ran while one was open for 4% of the time, Pallas kernels for 0%

commit v1 on v0

v1 whole, which is shorter than its diff:
```python
import jax
import jax.numpy as jnp
from jax import lax
from jax.experimental import pallas as pl
from jax.experimental.pallas import tpu as pltpu
from jax.sharding import PartitionSpec as P

F = 10
NJ = 16
G = 8
L = 128
C4 = 0.04 * 0.04
VMEM = pltpu.VMEM


def lanes():
    return lax.broadcasted_iota(jnp.int32, (1, 8, L), 2)


def sublanes(shape):
    return lax.broadcasted_iota(jnp.int32, shape, len(shape) - 2)


def load(nat, f, j0):
    return jnp.stack([nat[j0 + g, pl.ds(f, 8, stride=F), :] for g in range(G)])


def save(nat, f, j0, x):
    for g in range(G):
        nat[j0 + g, pl.ds(f, 8, stride=F), :] = x[g]


def put(t, f, j0, x):
    t[f + 1, j0 + 1 : j0 + 1 + G] = x
    if j0 == 0:
        t[f + 1, NJ + 1] = x[0]
    if j0 + G == NJ:
        t[f + 1, 0] = x[G - 1]
    if f == F - 1:
        t[0, j0 + 1 : j0 + 1 + G] = pltpu.roll(x, 1, 1)
    if f == 0:
        t[F + 1, j0 + 1 : j0 + 1 + G] = pltpu.roll(x, 7, 1)


def beside(u):
    first = lanes() == 0
    last = lanes() == L - 1
    right_of = pltpu.roll(u[: G + 1], 1, 2)
    left_of = pltpu.roll(u[1:], L - 1, 2)
    left = jnp.where(first, right_of[:G], right_of[1:])
    right = jnp.where(last, left_of[1:], left_of[:G])
    return left, right


def chunks():
    return [(f, j0) for f in range(F) for j0 in range(0, NJ, G)]


def weights(wn, f, j0):
    return load(wn[0], f, j0), load(wn[1], f, j0)


def masks(code):
    mc = code < 1.5
    mr = jnp.where(mc, code, code - 2.0) < 0.5
    return mr, mc


def to_t(nat, t):
    for f, j0 in chunks():
        put(t, f, j0, load(nat, f, j0))


def misfit_stage(tu, vn, code, wn, tout, out):
    for f, j0 in chunks():
        u = tu[f + 1, j0 : j0 + G + 2]
        left, right = beside(u)
        up = tu[f, j0 + 1 : j0 + 1 + G]
        down = tu[f + 2, j0 + 1 : j0 + 1 + G]
        mr, mc = masks(load(code, f, j0))
        cr, cc = weights(wn, f, j0)
        moved = (
            (1.0 - cr - cc) * u[1 : G + 1]
            + cr * jnp.where(mr, up, down)
            + cc * jnp.where(mc, left, right)
        )
        mis = load(vn, f, j0) - moved
        put(tout, f, j0, mis)
        if out is not None:
            save(out, f, j0, mis)


def sweep_stage(tin, tout, after):
    for f, j0 in chunks():
        u = tin[f + 1, j0 : j0 + G + 2]
        left, right = beside(u)
        up = tin[f, j0 + 1 : j0 + 1 + G]
        down = tin[f + 2, j0 + 1 : j0 + 1 + G]
        x = ((up + down) + (left + right)) + u[1 : G + 1]
        put(tout, f, j0, after(x, f, j0))


def smooth_stages(tin, tmp, pn, tout, inside):
    def mask(x, f, j0):
        return jnp.where(inside(f), x, 0.0)

    def scale(x, f, j0):
        return (load(pn, f, j0) * C4) * x

    sweep_stage(tin, tmp, mask)
    sweep_stage(tmp, tin, scale)
    sweep_stage(tin, tmp, mask)
    sweep_stage(tmp, tout, lambda x, f, j0: x)


def adjoint_stage(tw, code, wn, ta, tb, tc):
    first = lanes() == 0
    last = lanes() == L - 1
    for f, j0 in chunks():
        w = tw[f + 1, j0 + 1 : j0 + 1 + G]
        mr, mc = masks(load(code, f, j0))
        cr, cc = weights(wn, f, j0)
        along = cr * w
        lower = jnp.where(mr, along, 0.0)
        put(ta, f, j0, lower)
        put(tb, f, j0, along - lower)
        along = cc * w
        plus = jnp.where(mc, along, 0.0)
        put(tc, f, j0, plus)
        tc2 = along - plus
        put(tw2_ref[0], f, j0, tc2)
        base_ref[0][f, j0 : j0 + G] = (1.0 - cr - cc) * w
    for f, j0 in chunks():
        plus = tc[f + 1, j0 + 1 : j0 + G + 2]
        minus = tw2_ref[0][f + 1, j0 : j0 + G + 1]
        left_of = pltpu.roll(plus, L - 1, 2)
        right_of = pltpu.roll(minus, 1, 2)
        cols = jnp.where(last, left_of[1:], left_of[:G]) + jnp.where(
            first, right_of[:G], right_of[1:]
        )
        rows = ta[f + 2, j0 + 1 : j0 + 1 + G] + tb[f, j0 + 1 : j0 + 1 + G]
        base_ref[0][f, j0 : j0 + G] = base_ref[0][f, j0 : j0 + G] + rows + cols


tw2_ref = [None]
base_ref = [None]


def parity():
    return lax.axis_index("tm") % 2


def code_rows(codes, step):
    c = codes[step].astype(jnp.float32)
    return [jnp.broadcast_to(c[:, j : j + 1], (8, L)) for j in range(NJ)]


def pack_kernel(inc, prec, edge, codes, bulk_o, bulk_e, up, dn, sems):
    even = parity() == 0

    def forward(dst):
        return [pltpu.make_async_copy(inc.at[1], dst.at[pl.ds(0, 64)], sems.at[0])]

    def backward(dst):
        return [
            pltpu.make_async_copy(inc.at[0], dst.at[pl.ds(0, 64)], sems.at[1]),
            pltpu.make_async_copy(prec.at[0], dst.at[pl.ds(64, 64)], sems.at[2]),
        ]

    def start(fwd, bwd):
        for c in forward(fwd) + backward(bwd):
            c.start()

    @pl.when(even)
    def _():
        start(bulk_e, bulk_o)

    @pl.when(jnp.logical_not(even))
    def _():
        start(bulk_o, bulk_e)

    row = sublanes((8, L))
    rows0 = code_rows(codes, 0)
    rows1 = code_rows(codes, 1)
    for j in range(NJ):
        cols = pl.ds(j * L, L)
        bulk_o[128:136, cols] = rows0[j]
        bulk_e[128:136, cols] = rows0[j]
        inc0t, inc0b, inc1t, inc1b, p0t, p0b, p1t, p1b, crt, crb, cct, ccb = [
            edge[k, :, cols] for k in range(12)
        ]
        c0t = jnp.broadcast_to(rows0[j][0:1], (8, L))
        c0b = jnp.broadcast_to(rows0[j][7:8], (8, L))
        c1t = jnp.broadcast_to(rows1[j][0:1], (8, L))
        c1b = jnp.broadcast_to(rows1[j][7:8], (8, L))
        up[0:8, cols] = jnp.where(row < 2, c0b, inc0b)
        up[8:16, cols] = jnp.where(row < 2, c1b, inc1b)
        up[16:24, cols] = jnp.where(row < 3, pltpu.roll(p0b, 3, 0), crb)
        up[24:32, cols] = jnp.where(row < 3, pltpu.roll(p1b, 3, 0), ccb)
        dn[0:8, cols] = jnp.where(row > 5, c0t, inc0t)
        dn[8:16, cols] = jnp.where(row > 5, c1t, inc1t)
        dn[16:24, cols] = jnp.where(row > 4, pltpu.roll(p0t, 5, 0), crt)
        dn[24:32, cols] = jnp.where(row > 4, pltpu.roll(p1t, 5, 0), cct)

    @pl.when(even)
    def _():
        for c in forward(bulk_e) + backward(bulk_o):
            c.wait()

    @pl.when(jnp.logical_not(even))
    def _():
        for c in forward(bulk_o) + backward(bulk_e):
            c.wait()


def pack_body(inc, prec, cr, cc, codes, bulk_o, bulk_e, up, dn, edge, sems, esems):
    top, bottom = pl.ds(0, 8), pl.ds(56, 8)
    srcs = []
    for a in (inc.at[0], inc.at[1], prec.at[0], prec.at[1], cr, cc):
        srcs += [a.at[top], a.at[bottom]]
    copies = [pltpu.make_async_copy(s, edge.at[k], esems.at[k]) for k, s in enumerate(srcs)]
    for c in copies:
        c.start()
    for c in copies:
        c.wait()
    pack_kernel(inc, prec, edge, codes, bulk_o, bulk_e, up, dn, sems)


def pack(inc, prec, cr, cc, codes):
    any_spec = pl.BlockSpec(memory_space=pl.ANY)
    vmem = pl.BlockSpec(memory_space=VMEM)
    f32 = lambda *s: jax.ShapeDtypeStruct(s, jnp.float32)
    return pl.pallas_call(
        pack_body,
        in_specs=[any_spec] * 4 + [vmem],
        out_specs=[vmem] * 4,
        out_shape=[f32(136, 2048), f32(136, 2048), f32(32, 2048), f32(32, 2048)],
        scratch_shapes=[
            VMEM((12, 8, 2048), jnp.float32),
            pltpu.SemaphoreType.DMA((3,)),
            pltpu.SemaphoreType.DMA((12,)),
        ],
        compiler_params=pltpu.CompilerParams(vmem_limit_bytes=12 << 20),
        name="pack",
    )(inc, prec, cr, cc, codes)


def corner_body(up, dn, cor_o, cor_e):
    even = parity() == 0
    row = sublanes((8, 2048))

    def forward(dst):
        dst[0:8, :] = up[8:16, :]
        dst[8:16, :] = dn[8:16, :]
        dst[16:24, :] = up[8:16, :]

    def backward(dst):
        dst[0:8, :] = up[0:8, :]
        dst[8:16, :] = dn[0:8, :]
        dst[16:24, :] = jnp.where(row < 4, up[16:24, :], dn[16:24, :])

    @pl.when(even)
    def _():
        forward(cor_e)
        backward(cor_o)

    @pl.when(jnp.logical_not(even))
    def _():
        forward(cor_o)
        backward(cor_e)


def corner(up, dn):
    vmem = pl.BlockSpec(memory_space=VMEM)
    f32 = lambda *s: jax.ShapeDtypeStruct(s, jnp.float32)
    return pl.pallas_call(
        corner_body,
        in_specs=[vmem] * 2,
        out_specs=[vmem] * 2,
        out_shape=[f32(24, 2048), f32(24, 2048)],
        compiler_params=pltpu.CompilerParams(vmem_limit_bytes=4 << 20),
        name="corner",
    )(up, dn)


def main_body(
    inc, prec, cr, cc, codes, up, dn, bulk_o, bulk_e, cor_o, cor_e, mis, adj,
    n_prev, n_inc0, n_inc1, n_next, n_p0, n_p1, n_pn, n_cr, n_cc, n_c0, n_c1, n_cn,
    n_m0, n_m1, n_a0, n_a1,
    tu, ta, tb, tw1, tx, ty, base1, base2, isem, osem,
):
    even = parity() == 0
    slab = lax.axis_index("space")
    own = [(inc.at[0], n_inc0), (inc.at[1], n_inc1), (prec.at[0], n_p0), (prec.at[1], n_p1), (cr, n_cr), (cc, n_cc)]

    def copies(k):
        src, dst = own[k]
        return [
            pltpu.make_async_copy(
                src.at[:, pl.ds(j * L, L)], dst.at[j, pl.ds(8, 64)], isem.at[k * NJ + j]
            )
            for j in range(NJ)
        ]

    for k in range(6):
        for c in copies(k):
            c.start()

    def blk(ref, r, j):
        return ref[r : r + 8, j * L : (j + 1) * L]

    def spread(dst, j, at, x):
        dst[j, at : at + 8] = jnp.broadcast_to(x, (8, L))

    def halo(dst, j, top, bottom):
        dst[j, 0:8] = top
        dst[j, 72:80] = bottom

    rows0 = code_rows(codes, 0)
    rows1 = code_rows(codes, 1)
    for j in range(NJ):
        for n_c, rows, r in ((n_c0, rows0, 0), (n_c1, rows1, 8)):
            for b in range(8):
                spread(n_c, j, 8 + 8 * b, rows[j][b : b + 1])
            spread(n_c, j, 0, blk(up, r, j)[0:1])
            spread(n_c, j, 72, blk(dn, r, j)[7:8])
        halo(n_inc0, j, blk(up, 0, j), blk(dn, 0, j))
        halo(n_inc1, j, blk(up, 8, j), blk(dn, 8, j))
        halo(n_cr, j, blk(up, 16, j), blk(dn, 16, j))
        halo(n_cc, j, blk(up, 24, j), blk(dn, 24, j))
        halo(n_p0, j, pltpu.roll(blk(up, 16, j), 5, 0), pltpu.roll(blk(dn, 16, j), 3, 0))
        halo(n_p1, j, pltpu.roll(blk(up, 24, j), 5, 0), pltpu.roll(blk(dn, 24, j), 3, 0))

    def previous(bulk, cor):
        for j in range(NJ):
            for b in range(8):
                n_prev[j, 8 + 8 * b : 16 + 8 * b] = blk(bulk, 8 * b, j)
            halo(n_prev, j, blk(cor, 0, j), blk(cor, 8, j))

    def following(bulk, cor):
        for j in range(NJ):
            for b in range(8):
                n_next[j, 8 + 8 * b : 16 + 8 * b] = blk(bulk, 8 * b, j)
                n_pn[j, 8 + 8 * b : 16 + 8 * b] = blk(bulk, 64 + 8 * b, j)
                spread(n_cn, j, 8 + 8 * b, bulk[128 + b : 129 + b, j * L : (j + 1) * L])
            halo(n_next, j, blk(cor, 0, j), blk(cor, 8, j))
            spread(n_cn, j, 0, blk(cor, 0, j)[0:1])
            spread(n_cn, j, 72, blk(cor, 8, j)[7:8])
            halo(n_pn, j, pltpu.roll(blk(cor, 16, j), 5, 0), pltpu.roll(blk(cor, 16, j), 3, 0))

    @pl.when(even)
    def _():
        previous(bulk_o, cor_o)
        following(bulk_e, cor_e)

    @pl.when(jnp.logical_not(even))
    def _():
        previous(bulk_e, cor_e)
        following(bulk_o, cor_o)

    for k in range(6):
        for c in copies(k):
            c.wait()

    sub = sublanes((1, 8, L))
    top_out = (sub == 0) & (slab == 0)
    bottom_out = (sub == 7) & (slab == lax.axis_size("space") - 1)

    def inside(f):
        bad = None
        if f < 8:
            bad = top_out
        if f >= 2:
            bad = bottom_out if bad is None else bad | bottom_out
        return jnp.logical_not(bad)

    outs = []

    def emit(nat, dst, base):
        for j in range(NJ):
            c = pltpu.make_async_copy(
                nat.at[j, pl.ds(8, 64)], dst.at[:, pl.ds(j * L, L)], osem.at[base + j]
            )
            c.start()
            outs.append(c)

    wn = (n_cr, n_cc)
    tw2_ref[0] = ty
    to_t(n_inc0, tu)
    misfit_stage(tu, n_inc1, n_c1, wn, ta, n_m1)
    emit(n_m1, mis.at[1], 0)
    smooth_stages(ta, tb, n_p1, tw1, inside)
    base_ref[0] = base1
    adjoint_stage(tw1, n_c1, wn, ta, tb, tx)
    to_t(n_prev, tu)
    misfit_stage(tu, n_inc0, n_c0, wn, ta, n_m0)
    emit(n_m0, mis.at[0], NJ)
    smooth_stages(ta, tb, n_p0, tx, inside)
    for f, j0 in chunks():
        save(n_a0, f, j0, tx[f + 1, j0 + 1 : j0 + 1 + G] - base1[f, j0 : j0 + G])
    emit(n_a0, adj.at[0], 2 * NJ)
    to_t(n_inc1, tu)
    misfit_stage(tu, n_next, n_cn, wn, ta, None)
    smooth_stages(ta, tb, n_pn, tu, inside)
    base_ref[0] = base2
    adjoint_stage(tu, n_cn, wn, ta, tb, tx)
    for f, j0 in chunks():
        save(n_a1, f, j0, tw1[f + 1, j0 + 1 : j0 + 1 + G] - base2[f, j0 : j0 + G])
    emit(n_a1, adj.at[1], 3 * NJ)
    for c in outs:
        c.wait()


def main(*args):
    any_spec = pl.BlockSpec(memory_space=pl.ANY)
    vmem = pl.BlockSpec(memory_space=VMEM)
    nat = VMEM((NJ, 80, L), jnp.float32)
    t = VMEM((F + 2, NJ + 2, 8, L), jnp.float32)
    base = VMEM((F, NJ, 8, L), jnp.float32)
    out = jax.ShapeDtypeStruct((2, 64, 2048), jnp.float32)
    return pl.pallas_call(
        main_body,
        in_specs=[any_spec] * 4 + [vmem] * 7,
        out_specs=[any_spec] * 2,
        out_shape=[out, out],
        scratch_shapes=[nat] * 16
        + [t] * 6
        + [base] * 2
        + [pltpu.SemaphoreType.DMA((6 * NJ,)), pltpu.SemaphoreType.DMA((4 * NJ,))],
        compiler_params=pltpu.CompilerParams(vmem_limit_bytes=40 << 20),
        name="main",
    )(*args)


def permute(x, rule):
    axes = ("tm", "space")
    nt, ns = lax.axis_size("tm"), lax.axis_size("space")
    pairs = []
    for t in range(nt):
        for s in range(ns):
            a, b = rule(t, s)
            if 0 <= a < nt and 0 <= b < ns:
                pairs.append((t * ns + s, a * ns + b))
    return lax.ppermute(x, axes, pairs)


def off_chip(t, s):
    return (t - 1 if t % 2 == 0 else t + 1), s


def on_chip(t, s):
    return (t + 1 if t % 2 == 0 else t - 1), s


def on_device(inc, prec, cr, cc, codes):
    bulk_o, bulk_e, up, dn = pack(inc, prec, cr, cc, codes)
    bulk_o = permute(bulk_o, off_chip)
    up = permute(up, lambda t, s: (t, s + 1))
    bulk_e = permute(bulk_e, on_chip)
    dn = permute(dn, lambda t, s: (t, s - 1))
    cor_o, cor_e = corner(up, dn)
    cor_e = permute(cor_e, on_chip)
    cor_o = permute(cor_o, off_chip)
    return tuple(main(inc, prec, cr, cc, codes, up, dn, bulk_o, bulk_e, cor_o, cor_e))


def solution(mesh):
    in_specs = (
        P("tm", "space", None),
        P("tm", "space", None),
        P("space", None),
        P("space", None),
        P("tm", "space", None),
    )
    out_specs = (P("tm", "space", None), P("tm", "space", None))
    return jax.shard_map(
        on_device, mesh=mesh, in_specs=in_specs, out_specs=out_specs, check_vma=False
    )
```

time: 88.3 us -> 55.7 us (0.63)
  the two profiles are of different devices: /device:TPU:59 before, /device:TPU:6 now
where the time goes in v1:
time: 55.7 us; the launch traced here: 55.3 us
  starting transfers between devices  25.4 us (46%)
  Pallas kernels  12.7 us (23%)
  waiting for transfers between devices  11.2 us (20%)
  local copies, waits for them, and re-layouts  5.24 us (9%)
  between operations  0.77 us (1%)
    ppermute x6, starting transfers between devices, permute(): return lax.ppermute(x, axes, pairs)  25.4 us
    ppermute x6, waiting for transfers between devices, permute(): return lax.ppermute(x, axes, pairs)  11.2 us
    pallas_call x1, Pallas kernels, main(): pl.pallas_call(main_body, in_specs=[any_spec] * 4 + [vmem] * 7, out_specs...  11.1 us
    unnamed x20, local copies, waits for them, and re-layouts  5.24 us
    pallas_call x1, Pallas kernels, pack(): pl.pallas_call(pack_body, in_specs=[any_spec] * 4 + [vmem], out_specs=[vm...  1.51 us
  transfers between devices with their start and end apart: 6, of which 3 were waited for; matrix products, arithmetic and copies ran while one was open for 0% of the time, Pallas kernels for 0%

profile of v1, /device:TPU:6, one launch (start us, length us, event | category | flops | bytes accessed | tf_op | source)
XLA Modules:
  0.0 55.3 jit_solution(14032052689230666483)
XLA Ops:
  0.6 0.0 copy-start
  0.6 1.2 %copy-done = f32[2,64,2048]{2,1,0:T(8,128)S(1)} copy-done((f32[2,64,2048]{2,1,0:T(8,128)S(1)}, f32[2,64,2048]{2,1,0:T(8,128)}, u32[]{:S(2)}) %copy-start) | copy-done | bytes 1048600
  1.9 0.0 copy-start.2
  1.9 1.2 %copy-done.2 = f32[2,64,2048]{2,1,0:T(8,128)S(1)} copy-done((f32[2,64,2048]{2,1,0:T(8,128)S(1)}, f32[2,64,2048]{2,1,0:T(8,128)}, u32[]{:S(2)}) %copy-start.2) | copy-done | bytes 1048600
  3.1 0.0 copy-start.4
  3.1 1.0 %copy-done.4 = f32[64,2048]{1,0:T(8,128)S(1)} copy-done((f32[64,2048]{1,0:T(8,128)S(1)}, f32[64,2048]{1,0:T(8,128)}, u32[]{:S(2)}) %copy-start.4) | copy-done | bytes 524312
  4.1 0.0 copy-start.6
  4.1 1.0 %copy-done.6 = f32[64,2048]{1,0:T(8,128)S(1)} copy-done((f32[64,2048]{1,0:T(8,128)S(1)}, f32[64,2048]{1,0:T(8,128)}, u32[]{:S(2)}) %copy-start.6) | copy-done | bytes 524312
  5.2 0.0 copy-start.8
  5.2 0.7 %copy-done.8 = s32[2,8,16]{2,1,0:T(8,128)S(1)} copy-done((s32[2,8,16]{2,1,0:T(8,128)S(1)}, s32[2,8,16]{2,1,0:T(8,128)}, u32[]{:S(2)}) %copy-start.8) | copy-done | bytes 1048
  5.9 0.0 copy-start.1
  5.9 0.0 copy-start.3
  5.9 0.0 copy-start.5
  5.9 0.0 copy-start.7
  5.9 0.0 copy-start.9
  5.9 1.5 %pack.1 = (f32[136,2048]{1,0:T(8,128)S(1)}, f32[136,2048]{1,0:T(8,128)S(1)}, f32[32,2048]{1,0:T(8,128)S(1)}, f32[32,2048]{1,0:T(8,128)S(1)}) custom-call(f32[2,64,2048]{2,1,0:T(8,128)S(1)} %copy-done, f32[2,64,2048]{2,1,0:T(8,128)S(1)} %copy-done.2, f32[64,2048]{1,0:T(8,128)S(1)} %copy-done.4, f32[64,2048]{1,0:T(8,128)S(1)} %copy-done.6, ...), custom_call_target="tpu_custom_call" | custom-call | tf_op jit(solution)/shard_map/pack/pallas_call | solution.py:233
  7.4 5.7 %collective-permute-start.2 = (f32[136,2048]{1,0:T(8,128)S(1)}, f32[136,2048]{1,0:T(8,128)S(1)}, u32[]{:S(2)}, u32[]{:S(2)}) collective-permute-start(f32[136,2048]{1,0:T(8,128)S(1)} %get-tuple-element.10), channel_id=1, source_target_pairs={{16,32},{17,33},{18,34},{19,35},{20,36},{21,37},{22,38},{23,39},{2... | collective-permute-start | bytes 3342344 | tf_op jit(solution)/shard_map/ppermute | solution.py:444
  13.1 1.9 %collective-permute-start.3 = (f32[136,2048]{1,0:T(8,128)S(1)}, f32[136,2048]{1,0:T(8,128)S(1)}, u32[]{:S(2)}, u32[]{:S(2)}) collective-permute-start(f32[136,2048]{1,0:T(8,128)S(1)} %get-tuple-element.11), channel_id=1, source_target_pairs={{0,16},{1,17},{2,18},{3,19},{4,20},{5,21},{6,22},{7,23},{8,24},{9,... | collective-permute-start | bytes 3342344 | tf_op jit(solution)/shard_map/ppermute | solution.py:444
  15.0 4.3 %collective-permute-start = (f32[32,2048]{1,0:T(8,128)S(1)}, f32[32,2048]{1,0:T(8,128)S(1)}, u32[]{:S(2)}, u32[]{:S(2)}) collective-permute-start(f32[32,2048]{1,0:T(8,128)S(1)} %get-tuple-element.8), channel_id=1, source_target_pairs={{0,1},{1,2},{2,3},{3,4},{4,5},{5,6},{6,7},{7,8},{8,9},{9,10},{10,1... | collective-permute-start | bytes 786440 | tf_op jit(solution)/shard_map/ppermute | solution.py:444
  19.3 8.0 %collective-permute-start.1 = (f32[32,2048]{1,0:T(8,128)S(1)}, f32[32,2048]{1,0:T(8,128)S(1)}, u32[]{:S(2)}, u32[]{:S(2)}) collective-permute-start(f32[32,2048]{1,0:T(8,128)S(1)} %get-tuple-element.9), channel_id=1, source_target_pairs={{1,0},{2,1},{3,2},{4,3},{5,4},{6,5},{7,6},{8,7},{9,8},{10,9},{11,1... | collective-permute-start | bytes 786440 | tf_op jit(solution)/shard_map/ppermute | solution.py:444
  27.3 5.0 %collective-permute-done.up = f32[32,2048]{1,0:T(8,128)S(1)} collective-permute-done((f32[32,2048]{1,0:T(8,128)S(1)}, f32[32,2048]{1,0:T(8,128)S(1)}, u32[]{:S(2)}, u32[]{:S(2)}) %collective-permute-start) | collective-permute-done | bytes 262176 | tf_op jit(solution)/shard_map/ppermute | solution.py:444
  32.3 1.2 %collective-permute-done.1.dn = f32[32,2048]{1,0:T(8,128)S(1)} collective-permute-done((f32[32,2048]{1,0:T(8,128)S(1)}, f32[32,2048]{1,0:T(8,128)S(1)}, u32[]{:S(2)}, u32[]{:S(2)}) %collective-permute-start.1) | collective-permute-done | bytes 262176 | tf_op jit(solution)/shard_map/ppermute | solution.py:444
  33.5 3.7 %collective-permute-start.4 = (f32[24,2048]{1,0:T(8,128)S(1)}, f32[24,2048]{1,0:T(8,128)S(1)}, u32[]{:S(2)}, u32[]{:S(2)}) collective-permute-start(f32[24,2048]{1,0:T(8,128)S(1)} %get-tuple-element.12), channel_id=1, source_target_pairs={{16,32},{17,33},{18,34},{19,35},{20,36},{21,37},{22,38},{23,39},{2... | collective-permute-start | bytes 589832 | tf_op jit(solution)/shard_map/ppermute | solution.py:444
  37.2 1.9 %collective-permute-start.5 = (f32[24,2048]{1,0:T(8,128)S(1)}, f32[24,2048]{1,0:T(8,128)S(1)}, u32[]{:S(2)}, u32[]{:S(2)}) collective-permute-start(f32[24,2048]{1,0:T(8,128)S(1)} %get-tuple-element.13), channel_id=1, source_target_pairs={{0,16},{1,17},{2,18},{3,19},{4,20},{5,21},{6,22},{7,23},{8,24},{9,... | collective-permute-start | bytes 589832 | tf_op jit(solution)/shard_map/ppermute | solution.py:444
  39.1 5.0 %collective-permute-done.4.cor_o = f32[24,2048]{1,0:T(8,128)S(1)} collective-permute-done((f32[24,2048]{1,0:T(8,128)S(1)}, f32[24,2048]{1,0:T(8,128)S(1)}, u32[]{:S(2)}, u32[]{:S(2)}) %collective-permute-start.4) | collective-permute-done | bytes 196640 | tf_op jit(solution)/shard_map/ppermute | solution.py:444
  44.1 0.0 collective-permute-done.5.cor_e
  44.1 0.0 collective-permute-done.2.bulk_o
  44.1 0.0 collective-permute-done.3.bulk_e
  44.1 0.0 copy-done.1
  44.1 0.0 copy-done.3
  44.1 0.0 copy-done.5
  44.1 0.0 copy-done.7
  44.1 0.0 copy-done.9
  44.2 11.1 %main.1 = (f32[2,64,2048]{2,1,0:T(8,128)}, f32[2,64,2048]{2,1,0:T(8,128)}) custom-call(f32[2,64,2048]{2,1,0:T(8,128)S(1)} %copy-done.1, f32[2,64,2048]{2,1,0:T(8,128)S(1)} %copy-done.3, f32[64,2048]{1,0:T(8,128)S(1)} %copy-done.5, f32[64,2048]{1,0:T(8,128)S(1)} %copy-done.7, s32[2,8,16]{2,1,0:T(8,128)S(1)} %copy-done.9, ...), custom_call_target="tpu_custom_call" | custom-call | tf_op jit(solution)/shard_map/main/pallas_call | solution.py:421
  (1 shorter events, 0.0 us)
Async XLA Ops:
  0.6 1.2 %copy-start = (f32[2,64,2048]{2,1,0:T(8,128)S(1)}, f32[2,64,2048]{2,1,0:T(8,128)}, u32[]{:S(2)}) copy-start(f32[2,64,2048]{2,1,0:T(8,128)} %inc.3) | copy-start | bytes 3145732
  1.9 1.2 %copy-start.2 = (f32[2,64,2048]{2,1,0:T(8,128)S(1)}, f32[2,64,2048]{2,1,0:T(8,128)}, u32[]{:S(2)}) copy-start(f32[2,64,2048]{2,1,0:T(8,128)} %prec.3) | copy-start | bytes 3145732
  3.1 1.0 %copy-start.4 = (f32[64,2048]{1,0:T(8,128)S(1)}, f32[64,2048]{1,0:T(8,128)}, u32[]{:S(2)}) copy-start(f32[64,2048]{1,0:T(8,128)} %cr.3) | copy-start | bytes 1572868
  4.1 1.0 %copy-start.6 = (f32[64,2048]{1,0:T(8,128)S(1)}, f32[64,2048]{1,0:T(8,128)}, u32[]{:S(2)}) copy-start(f32[64,2048]{1,0:T(8,128)} %cc.3) | copy-start | bytes 1572868
  5.2 0.7 %copy-start.8 = (s32[2,8,16]{2,1,0:T(8,128)S(1)}, s32[2,8,16]{2,1,0:T(8,128)}, u32[]{:S(2)}) copy-start(s32[2,8,16]{2,1,0:T(8,128)} %codes.3) | copy-start | bytes 3076
  5.9 38.2 %copy-start.1 = (f32[2,64,2048]{2,1,0:T(8,128)S(1)}, f32[2,64,2048]{2,1,0:T(8,128)}, u32[]{:S(2)}) copy-start(f32[2,64,2048]{2,1,0:T(8,128)} %inc.3) | copy-start | bytes 3145732
  5.9 38.3 %copy-start.3 = (f32[2,64,2048]{2,1,0:T(8,128)S(1)}, f32[2,64,2048]{2,1,0:T(8,128)}, u32[]{:S(2)}) copy-start(f32[2,64,2048]{2,1,0:T(8,128)} %prec.3) | copy-start | bytes 3145732
  5.9 38.3 %copy-start.5 = (f32[64,2048]{1,0:T(8,128)S(1)}, f32[64,2048]{1,0:T(8,128)}, u32[]{:S(2)}) copy-start(f32[64,2048]{1,0:T(8,128)} %cr.3) | copy-start | bytes 1572868
  5.9 38.3 %copy-start.7 = (f32[64,2048]{1,0:T(8,128)S(1)}, f32[64,2048]{1,0:T(8,128)}, u32[]{:S(2)}) copy-start(f32[64,2048]{1,0:T(8,128)} %cc.3) | copy-start | bytes 1572868
  5.9 38.3 %copy-start.9 = (s32[2,8,16]{2,1,0:T(8,128)S(1)}, s32[2,8,16]{2,1,0:T(8,128)}, u32[]{:S(2)}) copy-start(s32[2,8,16]{2,1,0:T(8,128)} %codes.3) | copy-start | bytes 3076
  7.4 36.7 %collective-permute-start.2 = (f32[136,2048]{1,0:T(8,128)S(1)}, f32[136,2048]{1,0:T(8,128)S(1)}, u32[]{:S(2)}, u32[]{:S(2)}) collective-permute-start(f32[136,2048]{1,0:T(8,128)S(1)} %get-tuple-element.10), channel_id=1, source_target_pairs={{16,32},{17,33},{18,34},{19,35},{20,36},{21,37},{22,38},{23,39},{2... | collective-permute-start | bytes 3342344 | tf_op jit(solution)/shard_map/ppermute | solution.py:444
  13.1 31.0 %collective-permute-start.3 = (f32[136,2048]{1,0:T(8,128)S(1)}, f32[136,2048]{1,0:T(8,128)S(1)}, u32[]{:S(2)}, u32[]{:S(2)}) collective-permute-start(f32[136,2048]{1,0:T(8,128)S(1)} %get-tuple-element.11), channel_id=1, source_target_pairs={{0,16},{1,17},{2,18},{3,19},{4,20},{5,21},{6,22},{7,23},{8,24},{9,... | collective-permute-start | bytes 3342344 | tf_op jit(solution)/shard_map/ppermute | solution.py:444
  15.0 17.3 %collective-permute-start = (f32[32,2048]{1,0:T(8,128)S(1)}, f32[32,2048]{1,0:T(8,128)S(1)}, u32[]{:S(2)}, u32[]{:S(2)}) collective-permute-start(f32[32,2048]{1,0:T(8,128)S(1)} %get-tuple-element.8), channel_id=1, source_target_pairs={{0,1},{1,2},{2,3},{3,4},{4,5},{5,6},{6,7},{7,8},{8,9},{9,10},{10,1... | collective-permute-start | bytes 786440 | tf_op jit(solution)/shard_map/ppermute | solution.py:444
  19.3 14.2 %collective-permute-start.1 = (f32[32,2048]{1,0:T(8,128)S(1)}, f32[32,2048]{1,0:T(8,128)S(1)}, u32[]{:S(2)}, u32[]{:S(2)}) collective-permute-start(f32[32,2048]{1,0:T(8,128)S(1)} %get-tuple-element.9), channel_id=1, source_target_pairs={{1,0},{2,1},{3,2},{4,3},{5,4},{6,5},{7,6},{8,7},{9,8},{10,9},{11,1... | collective-permute-start | bytes 786440 | tf_op jit(solution)/shard_map/ppermute | solution.py:444
  33.5 10.6 %collective-permute-start.4 = (f32[24,2048]{1,0:T(8,128)S(1)}, f32[24,2048]{1,0:T(8,128)S(1)}, u32[]{:S(2)}, u32[]{:S(2)}) collective-permute-start(f32[24,2048]{1,0:T(8,128)S(1)} %get-tuple-element.12), channel_id=1, source_target_pairs={{16,32},{17,33},{18,34},{19,35},{20,36},{21,37},{22,38},{23,39},{2... | collective-permute-start | bytes 589832 | tf_op jit(solution)/shard_map/ppermute | solution.py:444
  37.2 6.9 %collective-permute-start.5 = (f32[24,2048]{1,0:T(8,128)S(1)}, f32[24,2048]{1,0:T(8,128)S(1)}, u32[]{:S(2)}, u32[]{:S(2)}) collective-permute-start(f32[24,2048]{1,0:T(8,128)S(1)} %get-tuple-element.13), channel_id=1, source_target_pairs={{0,16},{1,17},{2,18},{3,19},{4,20},{5,21},{6,22},{7,23},{8,24},{9,... | collective-permute-start | bytes 589832 | tf_op jit(solution)/shard_map/ppermute | solution.py:444

commit v2 on v1

v2 whole, which is shorter than its diff:
```python
import jax
import jax.numpy as jnp
from jax import lax
from jax.experimental import pallas as pl
from jax.experimental.pallas import tpu as pltpu
from jax.sharding import PartitionSpec as P


F = 10
NJ = 16
G = 4
L = 128
C4 = 0.04 * 0.04
VMEM = pltpu.VMEM


def lanes():
    return lax.broadcasted_iota(jnp.int32, (1, 8, L), 2)


def sublanes(shape):
    return lax.broadcasted_iota(jnp.int32, shape, len(shape) - 2)


def load(nat, f, j0, n):
    return jnp.stack([nat[(j0 + g) % NJ, pl.ds(f, 8, stride=F), :] for g in range(n)])


def save(nat, f, j0, x):
    for g in range(G):
        nat[j0 + g, pl.ds(f, 8, stride=F), :] = x[g]


def load_t(t, f, j0, n):
    parts = []
    if j0 < 0:
        parts.append(t[f, NJ - 1 : NJ])
    parts.append(t[f, max(j0, 0) : min(j0 + n, NJ)])
    if j0 + n > NJ:
        parts.append(t[f, 0:1])
    return parts[0] if len(parts) == 1 else jnp.concatenate(parts, axis=0)


def beside(u):
    first = lanes() == 0
    last = lanes() == L - 1
    right_of = pltpu.roll(u[: G + 1], 1, 2)
    left_of = pltpu.roll(u[1:], L - 1, 2)
    left = jnp.where(first, right_of[:G], right_of[1:])
    right = jnp.where(last, left_of[1:], left_of[:G])
    return left, right


def masks(code):
    mc = code < 1.5
    mr = jnp.where(mc, code, code - 2.0) < 0.5
    return mr, mc


def stencil(get, visit):
    for j0 in range(0, NJ, G):
        above = pltpu.roll(get(F - 1, j0, G), 1, 1)
        wide = get(0, j0 - 1, G + 2)
        for f in range(F):
            if f < F - 1:
                after = get(f + 1, j0 - 1, G + 2)
                below = after[1 : G + 1]
            else:
                after = None
                below = pltpu.roll(get(0, j0, G), 7, 1)
            visit(f, j0, wide, above, below)
            above = wide[1 : G + 1]
            wide = after


def misfit_stage(un, vn, code, wn, tout, out):
    def visit(f, j0, u, up, down):
        left, right = beside(u)
        mr, mc = masks(load(code, f, j0, G))
        cr, cc = load(wn[0], f, j0, G), load(wn[1], f, j0, G)
        moved = (
            (1.0 - cr - cc) * u[1 : G + 1]
            + cr * jnp.where(mr, up, down)
            + cc * jnp.where(mc, left, right)
        )
        mis = load(vn, f, j0, G) - moved
        tout[f, j0 : j0 + G] = mis
        if out is not None:
            save(out, f, j0, mis)

    stencil(lambda f, j0, n: load(un, f, j0, n), visit)


def sweep_stage(tin, tout, after):
    def visit(f, j0, u, up, down):
        left, right = beside(u)
        x = ((up + down) + (left + right)) + u[1 : G + 1]
        tout[f, j0 : j0 + G] = after(x, f, j0)

    stencil(lambda f, j0, n: load_t(tin, f, j0, n), visit)


def smooth_stages(tin, tmp, pn, tout, inside):
    def mask(x, f, j0):
        return jnp.where(inside(f), x, 0.0)

    def scale(x, f, j0):
        return (load(pn, f, j0, G) * C4) * x

    sweep_stage(tin, tmp, mask)
    sweep_stage(tmp, tin, scale)
    sweep_stage(tin, tmp, mask)
    sweep_stage(tmp, tout, lambda x, f, j0: x)


def adjoint_stage(tw, code, wn, emit):
    first = lanes() == 0
    last = lanes() == L - 1

    def pieces(f, j0):
        w = load_t(tw, f, j0 - 1, G + 2)
        mr, mc = masks(load(code, f, j0 - 1, G + 2))
        mr = mr[1 : G + 1]
        cr = load(wn[0], f, j0, G)
        cc = load(wn[1], f, j0 - 1, G + 2)
        mid = w[1 : G + 1]
        rows = cr * mid
        lower = jnp.where(mr, rows, 0.0)
        cols = cc * w
        plus = pltpu.roll(jnp.where(mc, cols, 0.0)[1:], L - 1, 2)
        minus = pltpu.roll(jnp.where(mc, 0.0, cols)[: G + 1], 1, 2)
        image = (
            (1.0 - cr - cc[1 : G + 1]) * mid
            + jnp.where(last, plus[1:], plus[:G])
            + jnp.where(first, minus[:G], minus[1:])
        )
        return image, lower, rows - lower

    def upper_only(f, j0):
        mr, _ = masks(load(code, f, j0, G))
        return jnp.where(mr, 0.0, load(wn[0], f, j0, G) * load_t(tw, f, j0, G))

    for j0 in range(0, NJ, G):
        above = pltpu.roll(upper_only(F - 1, j0), 1, 1)
        image, lower, upper = pieces(0, j0)
        lower0 = pltpu.roll(lower, 7, 1)
        for f in range(F):
            if f < F - 1:
                after = pieces(f + 1, j0)
                below = after[1]
            else:
                after = None
                below = lower0
            emit(f, j0, image + (above + below))
            above = upper
            if after is not None:
                image, lower, upper = after


def parity():
    return lax.axis_index("tm") % 2


def code_rows(codes, step):
    c = codes[step].astype(jnp.float32)
    return [jnp.broadcast_to(c[:, j : j + 1], (8, L)) for j in range(NJ)]


def pack_kernel(copies, inc, prec, edge, codes, bulk_o, bulk_e, up, dn, sems):
    even = parity() == 0

    def forward(dst):
        return [pltpu.make_async_copy(inc.at[1], dst.at[pl.ds(0, 64)], sems.at[0])]

    def backward(dst):
        return [
            pltpu.make_async_copy(inc.at[0], dst.at[pl.ds(0, 64)], sems.at[1]),
            pltpu.make_async_copy(prec.at[0], dst.at[pl.ds(64, 64)], sems.at[2]),
        ]

    def start(fwd, bwd):
        for c in forward(fwd) + backward(bwd):
            c.start()

    @pl.when(even)
    def _():
        start(bulk_e, bulk_o)

    @pl.when(jnp.logical_not(even))
    def _():
        start(bulk_o, bulk_e)

    for c in copies:
        c.wait()
    row = sublanes((8, L))
    rows0 = code_rows(codes, 0)
    rows1 = code_rows(codes, 1)
    for j in range(NJ):
        cols = pl.ds(j * L, L)
        bulk_o[128:136, cols] = rows0[j]
        bulk_e[128:136, cols] = rows0[j]
        inc0t, inc0b, inc1t, inc1b, p0t, p0b, p1t, p1b, crt, crb, cct, ccb = [
            edge[k, :, cols] for k in range(12)
        ]
        c0t = jnp.broadcast_to(rows0[j][0:1], (8, L))
        c0b = jnp.broadcast_to(rows0[j][7:8], (8, L))
        c1t = jnp.broadcast_to(rows1[j][0:1], (8, L))
        c1b = jnp.broadcast_to(rows1[j][7:8], (8, L))
        up[0:8, cols] = jnp.where(row < 2, c0b, inc0b)
        up[8:16, cols] = jnp.where(row < 2, c1b, inc1b)
        up[16:24, cols] = jnp.where(row < 3, pltpu.roll(p0b, 3, 0), crb)
        up[24:32, cols] = jnp.where(row < 3, pltpu.roll(p1b, 3, 0), ccb)
        dn[0:8, cols] = jnp.where(row > 5, c0t, inc0t)
        dn[8:16, cols] = jnp.where(row > 5, c1t, inc1t)
        dn[16:24, cols] = jnp.where(row > 4, pltpu.roll(p0t, 5, 0), crt)
        dn[24:32, cols] = jnp.where(row > 4, pltpu.roll(p1t, 5, 0), cct)

    @pl.when(even)
    def _():
        for c in forward(bulk_e) + backward(bulk_o):
            c.wait()

    @pl.when(jnp.logical_not(even))
    def _():
        for c in forward(bulk_o) + backward(bulk_e):
            c.wait()


def pack_body(inc, prec, cr, cc, codes_hbm, bulk_o, bulk_e, up, dn, codes, edge, sems, esems):
    top, bottom = pl.ds(0, 8), pl.ds(56, 8)
    srcs = []
    for a in (inc.at[0], inc.at[1], prec.at[0], prec.at[1], cr, cc):
        srcs += [a.at[top], a.at[bottom]]
    copies = [pltpu.make_async_copy(codes_hbm, codes, esems.at[12])]
    copies += [pltpu.make_async_copy(s, edge.at[k], esems.at[k]) for k, s in enumerate(srcs)]
    for c in copies:
        c.start()
    pack_kernel(copies, inc, prec, edge, codes, bulk_o, bulk_e, up, dn, sems)


def pack(inc, prec, cr, cc, codes):
    any_spec = pl.BlockSpec(memory_space=pltpu.HBM)
    vmem = pl.BlockSpec(memory_space=VMEM)
    f32 = lambda *s: jax.ShapeDtypeStruct(s, jnp.float32)
    return pl.pallas_call(
        pack_body,
        in_specs=[any_spec] * 5,
        out_specs=[vmem] * 4,
        out_shape=[f32(136, 2048), f32(160, 2048), f32(32, 2048), f32(32, 2048)],
        scratch_shapes=[
            VMEM((2, 8, 16), jnp.int32),
            VMEM((12, 8, 2048), jnp.float32),
            pltpu.SemaphoreType.DMA((3,)),
            pltpu.SemaphoreType.DMA((13,)),
        ],
        compiler_params=pltpu.CompilerParams(vmem_limit_bytes=12 << 20),
        name="pack",
    )(*(pltpu.with_memory_space_constraint(a, pltpu.HBM) for a in (inc, prec, cr, cc, codes)))


def corner_body(up, dn, bulk_in, cor_o, bulk_e):
    del bulk_in
    cor_e = bulk_e.at[136:160]
    even = parity() == 0
    row = sublanes((8, 2048))

    def forward(dst):
        dst[0:8, :] = up[8:16, :]
        dst[8:16, :] = dn[8:16, :]
        dst[16:24, :] = up[8:16, :]

    def backward(dst):
        dst[0:8, :] = up[0:8, :]
        dst[8:16, :] = dn[0:8, :]
        dst[16:24, :] = jnp.where(row < 4, up[16:24, :], dn[16:24, :])

    @pl.when(even)
    def _():
        forward(cor_e)
        backward(cor_o)

    @pl.when(jnp.logical_not(even))
    def _():
        forward(cor_o)
        backward(cor_e)


def corner(up, dn, bulk_e):
    vmem = pl.BlockSpec(memory_space=VMEM)
    f32 = lambda *s: jax.ShapeDtypeStruct(s, jnp.float32)
    return pl.pallas_call(
        corner_body,
        in_specs=[vmem] * 2 + [pl.BlockSpec(memory_space=pl.ANY)],
        out_specs=[vmem] * 2,
        out_shape=[f32(24, 2048), f32(160, 2048)],
        input_output_aliases={2: 1},
        compiler_params=pltpu.CompilerParams(vmem_limit_bytes=8 << 20),
        name="corner",
    )(up, dn, bulk_e)


def blk(ref, r, j):
    return ref[r : r + 8, j * L : (j + 1) * L]


def spread(dst, j, at, x):
    dst[j, at : at + 8] = jnp.broadcast_to(x, (8, L))


def halo(dst, j, top, bottom):
    dst[j, 0:8] = top
    dst[j, 72:80] = bottom


def fetch(pairs, sem):
    copies = [
        pltpu.make_async_copy(
            src.at[:, pl.ds(j * L, L)], dst.at[j, pl.ds(8, 64)], sem.at[k * NJ + j]
        )
        for k, (src, dst) in enumerate(pairs)
        for j in range(NJ)
    ]
    for c in copies:
        c.start()
    return copies


def emit_out(nat, dst, sem, base):
    copies = [
        pltpu.make_async_copy(
            nat.at[j, pl.ds(8, 64)], dst.at[:, pl.ds(j * L, L)], sem.at[base + j]
        )
        for j in range(NJ)
    ]
    for c in copies:
        c.start()
    return copies


def inside_rows():
    slab = lax.axis_index("space")
    sub = sublanes((1, 8, L))
    top_out = (sub == 0) & (slab == 0)
    bottom_out = (sub == 7) & (slab == lax.axis_size("space") - 1)

    def inside(f):
        bad = None
        if f < 8:
            bad = top_out
        if f >= 2:
            bad = bottom_out if bad is None else bad | bottom_out
        return jnp.logical_not(bad)

    return inside


def own_codes(codes, step, n_c, up, dn, r):
    rows = code_rows(codes, step)
    for j in range(NJ):
        for b in range(8):
            spread(n_c, j, 8 + 8 * b, rows[j][b : b + 1])
        spread(n_c, j, 0, blk(up, r, j)[0:1])
        spread(n_c, j, 72, blk(dn, r, j)[7:8])


def last_body(
    inc, prec, cr, cc, codes, up, dn, mis, w_out, image_out,
    n_inc0, n_inc1, n_p1, n_cr, n_cc, n_c1, n_m1, ta, tb, tw, isem, osem,
):
    copies = fetch(
        [(inc.at[0], n_inc0), (inc.at[1], n_inc1), (prec.at[1], n_p1), (cr, n_cr), (cc, n_cc)], isem
    )
    own_codes(codes, 1, n_c1, up, dn, 8)
    for j in range(NJ):
        halo(n_inc0, j, blk(up, 0, j), blk(dn, 0, j))
        halo(n_inc1, j, blk(up, 8, j), blk(dn, 8, j))
        halo(n_cr, j, blk(up, 16, j), blk(dn, 16, j))
        halo(n_cc, j, blk(up, 24, j), blk(dn, 24, j))
        halo(n_p1, j, pltpu.roll(blk(up, 24, j), 5, 0), pltpu.roll(blk(dn, 24, j), 3, 0))
    for c in copies:
        c.wait()
    wn = (n_cr, n_cc)
    inside = inside_rows()
    misfit_stage(n_inc0, n_inc1, n_c1, wn, ta, n_m1)
    outs = emit_out(n_m1, mis.at[1], osem, 0)
    smooth_stages(ta, tb, n_p1, tw, inside)

    def emit(f, j0, image):
        image_out[f, j0 : j0 + G] = image
        w_out[f, j0 : j0 + G] = tw[f, j0 : j0 + G]

    adjoint_stage(tw, n_c1, wn, emit)
    for c in outs:
        c.wait()


def first_body(
    inc, prec, cr, cc, codes, up, dn, bulk_o, bulk_e, cor_o, w1, image1, mis_in,
    mis, adj,
    n_prev, n_inc0, n_inc1, n_next, n_p0, n_pn, n_cr, n_cc, n_c0, n_cn, n_m0, n_a0, n_a1,
    ta, tb, tw, isem, osem,
):
    del mis_in
    even = parity() == 0
    cor_e = bulk_e.at[136:160]
    copies = fetch(
        [(inc.at[0], n_inc0), (inc.at[1], n_inc1), (prec.at[0], n_p0), (cr, n_cr), (cc, n_cc)], isem
    )
    own_codes(codes, 0, n_c0, up, dn, 0)
    for j in range(NJ):
        halo(n_inc0, j, blk(up, 0, j), blk(dn, 0, j))
        halo(n_inc1, j, blk(up, 8, j), blk(dn, 8, j))
        halo(n_cr, j, blk(up, 16, j), blk(dn, 16, j))
        halo(n_cc, j, blk(up, 24, j), blk(dn, 24, j))
        halo(n_p0, j, pltpu.roll(blk(up, 16, j), 5, 0), pltpu.roll(blk(dn, 16, j), 3, 0))

    def previous(bulk, cor):
        for j in range(NJ):
            for b in range(8):
                n_prev[j, 8 + 8 * b : 16 + 8 * b] = blk(bulk, 8 * b, j)
            halo(n_prev, j, blk(cor, 0, j), blk(cor, 8, j))

    def following(bulk, cor):
        for j in range(NJ):
            for b in range(8):
                n_next[j, 8 + 8 * b : 16 + 8 * b] = blk(bulk, 8 * b, j)
                n_pn[j, 8 + 8 * b : 16 + 8 * b] = blk(bulk, 64 + 8 * b, j)
                spread(n_cn, j, 8 + 8 * b, bulk[128 + b : 129 + b, j * L : (j + 1) * L])
            halo(n_next, j, blk(cor, 0, j), blk(cor, 8, j))
            spread(n_cn, j, 0, blk(cor, 0, j)[0:1])
            spread(n_cn, j, 72, blk(cor, 8, j)[7:8])
            halo(n_pn, j, pltpu.roll(blk(cor, 16, j), 5, 0), pltpu.roll(blk(cor, 16, j), 3, 0))

    @pl.when(even)
    def _():
        previous(bulk_o, cor_o)
        following(bulk_e, cor_e)

    @pl.when(jnp.logical_not(even))
    def _():
        previous(bulk_e, cor_e)
        following(bulk_o, cor_o)

    for c in copies:
        c.wait()
    wn = (n_cr, n_cc)
    inside = inside_rows()
    misfit_stage(n_prev, n_inc0, n_c0, wn, ta, n_m0)
    outs = emit_out(n_m0, mis.at[0], osem, 0)
    smooth_stages(ta, tb, n_p0, tw, inside)
    for f in range(F):
        for j0 in range(0, NJ, G):
            save(n_a0, f, j0, tw[f, j0 : j0 + G] - image1[f, j0 : j0 + G])
    outs += emit_out(n_a0, adj.at[0], osem, NJ)
    misfit_stage(n_inc1, n_next, n_cn, wn, ta, None)
    smooth_stages(ta, tb, n_pn, tw, inside)
    adjoint_stage(
        tw, n_cn, wn, lambda f, j0, image: save(n_a1, f, j0, w1[f, j0 : j0 + G] - image)
    )
    outs += emit_out(n_a1, adj.at[1], osem, 2 * NJ)
    for c in outs:
        c.wait()


NAT = VMEM((NJ, 80, L), jnp.float32)
TFORM = VMEM((F, NJ, 8, L), jnp.float32)
ON_HBM = pl.BlockSpec(memory_space=pltpu.HBM)
ON_VMEM = pl.BlockSpec(memory_space=VMEM)
OUT = jax.ShapeDtypeStruct((2, 64, 2048), jnp.float32)


def last_step(*args):
    t = jax.ShapeDtypeStruct((F, NJ, 8, L), jnp.float32)
    return pl.pallas_call(
        last_body,
        in_specs=[ON_HBM] * 4 + [ON_VMEM] * 3,
        out_specs=[ON_HBM] + [ON_VMEM] * 2,
        out_shape=[OUT, t, t],
        scratch_shapes=[NAT] * 7
        + [TFORM] * 3
        + [pltpu.SemaphoreType.DMA((5 * NJ,)), pltpu.SemaphoreType.DMA((NJ,))],
        compiler_params=pltpu.CompilerParams(vmem_limit_bytes=24 << 20),
        name="last",
    )(*args)


def first_steps(*args):
    return pl.pallas_call(
        first_body,
        in_specs=[ON_HBM] * 4 + [ON_VMEM] * 8 + [ON_HBM],
        out_specs=[ON_HBM] * 2,
        out_shape=[OUT, OUT],
        scratch_shapes=[NAT] * 13
        + [TFORM] * 3
        + [pltpu.SemaphoreType.DMA((5 * NJ,)), pltpu.SemaphoreType.DMA((3 * NJ,))],
        input_output_aliases={12: 0},
        compiler_params=pltpu.CompilerParams(vmem_limit_bytes=24 << 20),
        name="first",
    )(*args)


def permute(x, rule):
    axes = ("tm", "space")
    nt, ns = lax.axis_size("tm"), lax.axis_size("space")
    pairs = []
    for t in range(nt):
        for s in range(ns):
            a, b = rule(t, s)
            if 0 <= a < nt and 0 <= b < ns:
                pairs.append((t * ns + s, a * ns + b))
    return lax.ppermute(x, axes, pairs)


def off_chip(t, s):
    return (t - 1 if t % 2 == 0 else t + 1), s


def on_chip(t, s):
    return (t + 1 if t % 2 == 0 else t - 1), s


def on_device(inc, prec, cr, cc, codes):
    bulk_o, bulk_e, up, dn = pack(inc, prec, cr, cc, codes)
    up = permute(up, lambda t, s: (t, s + 1))
    bulk_o = permute(bulk_o, off_chip)
    dn = permute(dn, lambda t, s: (t, s - 1))
    cor_o, bulk_e = corner(up, dn, bulk_e)
    cor_o = permute(cor_o, off_chip)
    bulk_e = permute(bulk_e, on_chip)
    mis, w1, image1 = last_step(inc, prec, cr, cc, codes, up, dn)
    return tuple(
        first_steps(
            inc, prec, cr, cc, codes, up, dn, bulk_o, bulk_e, cor_o, w1, image1, mis
        )
    )


def solution(mesh):
    in_specs = (
        P("tm", "space", None),
        P("tm", "space", None),
        P("space", None),
        P("space", None),
        P("tm", "space", None),
    )
    out_specs = (P("tm", "space", None), P("tm", "space", None))
    return jax.shard_map(
        on_device, mesh=mesh, in_specs=in_specs, out_specs=out_specs, check_vma=False
    )
```

time: 55.7 us -> 54.8 us (0.984)
  the two profiles are of different devices: /device:TPU:6 before, /device:TPU:59 now
where the time goes in v2:
time: 54.8 us; the launch traced here: 54.5 us
  starting transfers between devices  25.5 us (47%)
  Pallas kernels  15.3 us (28%)
  waiting for transfers between devices  13 us (24%)
  between operations  0.77 us (1%)
    ppermute x5, starting transfers between devices, permute(): return lax.ppermute(x, axes, pairs)  25.5 us
    ppermute x5, waiting for transfers between devices, permute(): return lax.ppermute(x, axes, pairs)  13 us
    pallas_call x1, Pallas kernels, first_steps(): pl.pallas_call(first_body, in_specs=[ON_HBM] * 4 + [ON_VMEM] * 8 + [ON_HB...  8.16 us
    pallas_call x1, Pallas kernels, last_step(): pl.pallas_call(last_body, in_specs=[ON_HBM] * 4 + [ON_VMEM] * 3, out_spec...  5.11 us
    pallas_call x1, Pallas kernels, pack(): pl.pallas_call(pack_body, in_specs=[any_spec] * 5, out_specs=[vmem] * 4,...  1.98 us
  transfers between devices with their start and end apart: 5, of which 3 were waited for; matrix products, arithmetic and copies ran while one was open for 0% of the time, Pallas kernels for 9%

profile of v2, /device:TPU:59, one launch (start us, length us, event | category | flops | bytes accessed | tf_op | source)
XLA Modules:
  0.0 54.5 jit_solution(15718628486884796822)
XLA Ops:
  0.6 0.0 copy-start.1
  0.6 0.0 copy-start.3
  0.6 2.0 %pack.1 = (f32[136,2048]{1,0:T(8,128)S(1)}, f32[160,2048]{1,0:T(8,128)S(1)}, f32[32,2048]{1,0:T(8,128)S(1)}, f32[32,2048]{1,0:T(8,128)S(1)}) custom-call(f32[2,64,2048]{2,1,0:T(8,128)} %inc.5, f32[2,64,2048]{2,1,0:T(8,128)} %prec.5, f32[64,2048]{1,0:T(8,128)} %cr.5, f32[64,2048]{1,0:T(8,128)} %cc.5, s32[2,8,16]{2,1,0:T(8,128)} %codes.3), custom_call_target="tpu_custom_call" | custom-call | tf_op jit(solution)/shard_map/pack/pallas_call | solution.py:245
  2.6 0.0 copy-start
  2.7 0.0 copy-start.2
  2.7 0.0 copy-start.4
  2.7 4.1 %collective-permute-start = (f32[32,2048]{1,0:T(8,128)S(1)}, f32[32,2048]{1,0:T(8,128)S(1)}, u32[]{:S(2)}, u32[]{:S(2)}) collective-permute-start(f32[32,2048]{1,0:T(8,128)S(1)} %get-tuple-element.11), channel_id=1, source_target_pairs={{0,1},{1,2},{2,3},{3,4},{4,5},{5,6},{6,7},{7,8},{8,9},{9,10},{10,1... | collective-permute-start | bytes 786440 | tf_op jit(solution)/shard_map/ppermute | solution.py:511
  6.8 8.6 %collective-permute-start.1 = (f32[32,2048]{1,0:T(8,128)S(1)}, f32[32,2048]{1,0:T(8,128)S(1)}, u32[]{:S(2)}, u32[]{:S(2)}) collective-permute-start(f32[32,2048]{1,0:T(8,128)S(1)} %get-tuple-element.12), channel_id=1, source_target_pairs={{1,0},{2,1},{3,2},{4,3},{5,4},{6,5},{7,6},{8,7},{9,8},{10,9},{11,1... | collective-permute-start | bytes 786440 | tf_op jit(solution)/shard_map/ppermute | solution.py:511
  15.4 3.9 %collective-permute-done.up = f32[32,2048]{1,0:T(8,128)S(1)} collective-permute-done((f32[32,2048]{1,0:T(8,128)S(1)}, f32[32,2048]{1,0:T(8,128)S(1)}, u32[]{:S(2)}, u32[]{:S(2)}) %collective-permute-start) | collective-permute-done | bytes 262176 | tf_op jit(solution)/shard_map/ppermute | solution.py:511
  19.3 0.9 %collective-permute-done.1.dn = f32[32,2048]{1,0:T(8,128)S(1)} collective-permute-done((f32[32,2048]{1,0:T(8,128)S(1)}, f32[32,2048]{1,0:T(8,128)S(1)}, u32[]{:S(2)}, u32[]{:S(2)}) %collective-permute-start.1) | collective-permute-done | bytes 262176 | tf_op jit(solution)/shard_map/ppermute | solution.py:511
  20.2 3.6 %collective-permute-start.3 = (f32[160,2048]{1,0:T(8,128)S(1)}, f32[160,2048]{1,0:T(8,128)S(1)}, u32[]{:S(2)}, u32[]{:S(2)}) collective-permute-start(f32[160,2048]{1,0:T(8,128)S(1)} %get-tuple-element.15), channel_id=1, source_target_pairs={{0,16},{1,17},{2,18},{3,19},{4,20},{5,21},{6,22},{7,23},{8,24},{9,... | collective-permute-start | bytes 3932168 | tf_op jit(solution)/shard_map/ppermute | solution.py:511
  23.8 3.1 %collective-permute-start.2 = (f32[136,2048]{1,0:T(8,128)S(1)}, f32[136,2048]{1,0:T(8,128)S(1)}, u32[]{:S(2)}, u32[]{:S(2)}) collective-permute-start(f32[136,2048]{1,0:T(8,128)S(1)} %get-tuple-element.13), channel_id=1, source_target_pairs={{16,32},{17,33},{18,34},{19,35},{20,36},{21,37},{22,38},{23,39},{2... | collective-permute-start | bytes 3342344 | tf_op jit(solution)/shard_map/ppermute | solution.py:511
  27.0 6.0 %collective-permute-start.4 = (f32[24,2048]{1,0:T(8,128)S(1)}, f32[24,2048]{1,0:T(8,128)S(1)}, u32[]{:S(2)}, u32[]{:S(2)}) collective-permute-start(f32[24,2048]{1,0:T(8,128)S(1)} %get-tuple-element.16), channel_id=1, source_target_pairs={{16,32},{17,33},{18,34},{19,35},{20,36},{21,37},{22,38},{23,39},{2... | collective-permute-start | bytes 589832 | tf_op jit(solution)/shard_map/ppermute | solution.py:511
  33.0 0.0 copy-done.1
  33.0 0.0 copy-done.3
  33.0 0.0 copy-done
  33.1 0.0 copy-done.2
  33.1 0.0 copy-done.4
  33.1 5.1 %last.1 = (f32[2,64,2048]{2,1,0:T(8,128)}, f32[10,16,8,128]{3,2,1,0:T(8,128)S(1)}, f32[10,16,8,128]{3,2,1,0:T(8,128)S(1)}) custom-call(f32[2,64,2048]{2,1,0:T(8,128)S(1)} %copy-done, f32[2,64,2048]{2,1,0:T(8,128)S(1)} %copy-done.1, f32[64,2048]{1,0:T(8,128)S(1)} %copy-done.2, f32[64,2048]{1,0:T(8,128)S(1)} %copy-done.3, s32[2,8,16]{2,1,0:T(8,128)S(1)} %copy-done.4, ...), custom_call_target="tpu_custom_call" | custom-call | tf_op jit(solution)/shard_map/last/pallas_call | solution.py:474
  38.2 8.2 %collective-permute-done.4.cor_o = f32[24,2048]{1,0:T(8,128)S(1)} collective-permute-done((f32[24,2048]{1,0:T(8,128)S(1)}, f32[24,2048]{1,0:T(8,128)S(1)}, u32[]{:S(2)}, u32[]{:S(2)}) %collective-permute-start.4) | collective-permute-done | bytes 196640 | tf_op jit(solution)/shard_map/ppermute | solution.py:511
  46.4 0.0 collective-permute-done.2.bulk_o
  46.4 0.0 collective-permute-done.3.bulk_e
  46.4 8.2 %first.1 = (f32[2,64,2048]{2,1,0:T(8,128)}, f32[2,64,2048]{2,1,0:T(8,128)}) custom-call(f32[2,64,2048]{2,1,0:T(8,128)S(1)} %copy-done, f32[2,64,2048]{2,1,0:T(8,128)S(1)} %copy-done.1, f32[64,2048]{1,0:T(8,128)S(1)} %copy-done.2, f32[64,2048]{1,0:T(8,128)S(1)} %copy-done.3, s32[2,8,16]{2,1,0:T(8,128)S(1)} %copy-done.4, ...), custom_call_target="tpu_custom_call", output_to_operand_aliasing={{0}: (12, {})} | custom-call | tf_op jit(solution)/shard_map/first/pallas_call | solution.py:488
  (1 shorter events, 0.0 us)
Async XLA Ops:
  0.6 32.4 %copy-start.1 = (f32[2,64,2048]{2,1,0:T(8,128)S(1)}, f32[2,64,2048]{2,1,0:T(8,128)}, u32[]{:S(2)}) copy-start(f32[2,64,2048]{2,1,0:T(8,128)} %prec.5) | copy-start | bytes 3145732
  0.6 32.4 %copy-start.3 = (f32[64,2048]{1,0:T(8,128)S(1)}, f32[64,2048]{1,0:T(8,128)}, u32[]{:S(2)}) copy-start(f32[64,2048]{1,0:T(8,128)} %cc.5) | copy-start | bytes 1572868
  2.6 30.4 %copy-start = (f32[2,64,2048]{2,1,0:T(8,128)S(1)}, f32[2,64,2048]{2,1,0:T(8,128)}, u32[]{:S(2)}) copy-start(f32[2,64,2048]{2,1,0:T(8,128)} %inc.5) | copy-start | bytes 3145732
  2.7 30.4 %copy-start.2 = (f32[64,2048]{1,0:T(8,128)S(1)}, f32[64,2048]{1,0:T(8,128)}, u32[]{:S(2)}) copy-start(f32[64,2048]{1,0:T(8,128)} %cr.5) | copy-start | bytes 1572868
  2.7 30.4 %copy-start.4 = (s32[2,8,16]{2,1,0:T(8,128)S(1)}, s32[2,8,16]{2,1,0:T(8,128)}, u32[]{:S(2)}) copy-start(s32[2,8,16]{2,1,0:T(8,128)} %codes.3) | copy-start | bytes 3076
  2.7 16.6 %collective-permute-start = (f32[32,2048]{1,0:T(8,128)S(1)}, f32[32,2048]{1,0:T(8,128)S(1)}, u32[]{:S(2)}, u32[]{:S(2)}) collective-permute-start(f32[32,2048]{1,0:T(8,128)S(1)} %get-tuple-element.11), channel_id=1, source_target_pairs={{0,1},{1,2},{2,3},{3,4},{4,5},{5,6},{6,7},{7,8},{8,9},{9,10},{10,1... | collective-permute-start | bytes 786440 | tf_op jit(solution)/shard_map/ppermute | solution.py:511
  6.8 13.4 %collective-permute-start.1 = (f32[32,2048]{1,0:T(8,128)S(1)}, f32[32,2048]{1,0:T(8,128)S(1)}, u32[]{:S(2)}, u32[]{:S(2)}) collective-permute-start(f32[32,2048]{1,0:T(8,128)S(1)} %get-tuple-element.12), channel_id=1, source_target_pairs={{1,0},{2,1},{3,2},{4,3},{5,4},{6,5},{7,6},{8,7},{9,8},{10,9},{11,1... | collective-permute-start | bytes 786440 | tf_op jit(solution)/shard_map/ppermute | solution.py:511
  20.2 26.2 %collective-permute-start.3 = (f32[160,2048]{1,0:T(8,128)S(1)}, f32[160,2048]{1,0:T(8,128)S(1)}, u32[]{:S(2)}, u32[]{:S(2)}) collective-permute-start(f32[160,2048]{1,0:T(8,128)S(1)} %get-tuple-element.15), channel_id=1, source_target_pairs={{0,16},{1,17},{2,18},{3,19},{4,20},{5,21},{6,22},{7,23},{8,24},{9,... | collective-permute-start | bytes 3932168 | tf_op jit(solution)/shard_map/ppermute | solution.py:511
  23.8 22.5 %collective-permute-start.2 = (f32[136,2048]{1,0:T(8,128)S(1)}, f32[136,2048]{1,0:T(8,128)S(1)}, u32[]{:S(2)}, u32[]{:S(2)}) collective-permute-start(f32[136,2048]{1,0:T(8,128)S(1)} %get-tuple-element.13), channel_id=1, source_target_pairs={{16,32},{17,33},{18,34},{19,35},{20,36},{21,37},{22,38},{23,39},{2... | collective-permute-start | bytes 3342344 | tf_op jit(solution)/shard_map/ppermute | solution.py:511
  27.0 19.4 %collective-permute-start.4 = (f32[24,2048]{1,0:T(8,128)S(1)}, f32[24,2048]{1,0:T(8,128)S(1)}, u32[]{:S(2)}, u32[]{:S(2)}) collective-permute-start(f32[24,2048]{1,0:T(8,128)S(1)} %get-tuple-element.16), channel_id=1, source_target_pairs={{16,32},{17,33},{18,34},{19,35},{20,36},{21,37},{22,38},{23,39},{2... | collective-permute-start | bytes 589832 | tf_op jit(solution)/shard_map/ppermute | solution.py:511

commit v3 on v2

--- a/solution.py
+++ b/solution.py
@@ -166,7 +166,7 @@
     return [jnp.broadcast_to(c[:, j : j + 1], (8, L)) for j in range(NJ)]
 
 
-def pack_kernel(copies, inc, prec, edge, codes, bulk_o, bulk_e, up, dn, sems):
+def pack_kernel(copies, inc, prec, edge, codes, bulk_o, bulk_e, pass_1, pass_2, sems):
     even = parity() == 0
 
     def forward(dst):
@@ -199,21 +199,33 @@
         cols = pl.ds(j * L, L)
         bulk_o[128:136, cols] = rows0[j]
         bulk_e[128:136, cols] = rows0[j]
-        inc0t, inc0b, inc1t, inc1b, p0t, p0b, p1t, p1b, crt, crb, cct, ccb = [
-            edge[k, :, cols] for k in range(12)
-        ]
-        c0t = jnp.broadcast_to(rows0[j][0:1], (8, L))
-        c0b = jnp.broadcast_to(rows0[j][7:8], (8, L))
-        c1t = jnp.broadcast_to(rows1[j][0:1], (8, L))
-        c1b = jnp.broadcast_to(rows1[j][7:8], (8, L))
-        up[0:8, cols] = jnp.where(row < 2, c0b, inc0b)
-        up[8:16, cols] = jnp.where(row < 2, c1b, inc1b)
-        up[16:24, cols] = jnp.where(row < 3, pltpu.roll(p0b, 3, 0), crb)
-        up[24:32, cols] = jnp.where(row < 3, pltpu.roll(p1b, 3, 0), ccb)
-        dn[0:8, cols] = jnp.where(row > 5, c0t, inc0t)
-        dn[8:16, cols] = jnp.where(row > 5, c1t, inc1t)
-        dn[16:24, cols] = jnp.where(row > 4, pltpu.roll(p0t, 5, 0), crt)
-        dn[24:32, cols] = jnp.where(row > 4, pltpu.roll(p1t, 5, 0), cct)
+
+    def edges(up, dn):
+        for j in range(NJ):
+            cols = pl.ds(j * L, L)
+            inc0t, inc0b, inc1t, inc1b, p0t, p0b, p1t, p1b, crt, crb, cct, ccb = [
+                edge[k, :, cols] for k in range(12)
+            ]
+            c0t = jnp.broadcast_to(rows0[j][0:1], (8, L))
+            c0b = jnp.broadcast_to(rows0[j][7:8], (8, L))
+            c1t = jnp.broadcast_to(rows1[j][0:1], (8, L))
+            c1b = jnp.broadcast_to(rows1[j][7:8], (8, L))
+            up[0:8, cols] = jnp.where(row < 2, c0b, inc0b)
+            up[8:16, cols] = jnp.where(row < 2, c1b, inc1b)
+            up[16:24, cols] = jnp.where(row < 3, pltpu.roll(p0b, 3, 0), crb)
+            up[24:32, cols] = jnp.where(row < 3, pltpu.roll(p1b, 3, 0), ccb)
+            dn[0:8, cols] = jnp.where(row > 5, c0t, inc0t)
+            dn[8:16, cols] = jnp.where(row > 5, c1t, inc1t)
+            dn[16:24, cols] = jnp.where(row > 4, pltpu.roll(p0t, 5, 0), crt)
+            dn[24:32, cols] = jnp.where(row > 4, pltpu.roll(p1t, 5, 0), cct)
+
+    @pl.when(even)
+    def _():
+        edges(pass_1, pass_2)
+
+    @pl.when(jnp.logical_not(even))
+    def _():
+        edges(pass_2, pass_1)
 
     @pl.when(even)
     def _():
@@ -226,7 +238,7 @@
             c.wait()
 
 
-def pack_body(inc, prec, cr, cc, codes_hbm, bulk_o, bulk_e, up, dn, codes, edge, sems, esems):
+def pack_body(inc, prec, cr, cc, codes_hbm, bulk_o, bulk_e, pass_1, pass_2, codes, edge, sems, esems):
     top, bottom = pl.ds(0, 8), pl.ds(56, 8)
     srcs = []
     for a in (inc.at[0], inc.at[1], prec.at[0], prec.at[1], cr, cc):
@@ -235,7 +247,7 @@
     copies += [pltpu.make_async_copy(s, edge.at[k], esems.at[k]) for k, s in enumerate(srcs)]
     for c in copies:
         c.start()
-    pack_kernel(copies, inc, prec, edge, codes, bulk_o, bulk_e, up, dn, sems)
+    pack_kernel(copies, inc, prec, edge, codes, bulk_o, bulk_e, pass_1, pass_2, sems)
 
 
 def pack(inc, prec, cr, cc, codes):
@@ -258,45 +270,49 @@
     )(*(pltpu.with_memory_space_constraint(a, pltpu.HBM) for a in (inc, prec, cr, cc, codes)))
 
 
-def corner_body(up, dn, bulk_in, cor_o, bulk_e):
+def corner_body(pass_1, pass_2, bulk_in, up, dn, cor_o, bulk_e):
     del bulk_in
     cor_e = bulk_e.at[136:160]
     even = parity() == 0
     row = sublanes((8, 2048))
 
-    def forward(dst):
+    def forward(up, dn, dst):
         dst[0:8, :] = up[8:16, :]
         dst[8:16, :] = dn[8:16, :]
         dst[16:24, :] = up[8:16, :]
 
-    def backward(dst):
+    def backward(up, dn, dst):
         dst[0:8, :] = up[0:8, :]
         dst[8:16, :] = dn[0:8, :]
         dst[16:24, :] = jnp.where(row < 4, up[16:24, :], dn[16:24, :])
 
+    def both(from_up, from_dn, fwd, bwd):
+        up[...] = from_up[...]
+        dn[...] = from_dn[...]
+        forward(from_up, from_dn, fwd)
+        backward(from_up, from_dn, bwd)
+
     @pl.when(even)
     def _():
-        forward(cor_e)
-        backward(cor_o)
+        both(pass_1, pass_2, cor_e, cor_o)
 
     @pl.when(jnp.logical_not(even))
     def _():
-        forward(cor_o)
-        backward(cor_e)
-
-
-def corner(up, dn, bulk_e):
+        both(pass_2, pass_1, cor_o, cor_e)
+
+
+def corner(pass_1, pass_2, bulk_e):
     vmem = pl.BlockSpec(memory_space=VMEM)
     f32 = lambda *s: jax.ShapeDtypeStruct(s, jnp.float32)
     return pl.pallas_call(
         corner_body,
         in_specs=[vmem] * 2 + [pl.BlockSpec(memory_space=pl.ANY)],
-        out_specs=[vmem] * 2,
-        out_shape=[f32(24, 2048), f32(160, 2048)],
-        input_output_aliases={2: 1},
+        out_specs=[vmem] * 4,
+        out_shape=[f32(32, 2048), f32(32, 2048), f32(24, 2048), f32(160, 2048)],
+        input_output_aliases={2: 3},
         compiler_params=pltpu.CompilerParams(vmem_limit_bytes=8 << 20),
         name="corner",
-    )(up, dn, bulk_e)
+    )(pass_1, pass_2, bulk_e)
 
 
 def blk(ref, r, j):
@@ -312,17 +328,10 @@
     dst[j, 72:80] = bottom
 
 
-def fetch(pairs, sem):
-    copies = [
-        pltpu.make_async_copy(
-            src.at[:, pl.ds(j * L, L)], dst.at[j, pl.ds(8, 64)], sem.at[k * NJ + j]
-        )
-        for k, (src, dst) in enumerate(pairs)
-        for j in range(NJ)
-    ]
-    for c in copies:
-        c.start()
-    return copies
+def fill(src, dst):
+    for j in range(NJ):
+        for b in range(8):
+            dst[j, 8 + 8 * b : 16 + 8 * b] = src[8 * b : 8 * b + 8, j * L : (j + 1) * L]
 
 
 def emit_out(nat, dst, sem, base):
@@ -364,12 +373,13 @@
 
 
 def last_body(
-    inc, prec, cr, cc, codes, up, dn, mis, w_out, image_out,
-    n_inc0, n_inc1, n_p1, n_cr, n_cc, n_c1, n_m1, ta, tb, tw, isem, osem,
+    inc, prec, cr, cc, codes, up, dn, mis, w_out, image_out, n_inc0, n_inc1, n_cr, n_cc,
+    n_p1, n_c1, n_m1, ta, tb, tw, osem,
 ):
-    copies = fetch(
-        [(inc.at[0], n_inc0), (inc.at[1], n_inc1), (prec.at[1], n_p1), (cr, n_cr), (cc, n_cc)], isem
-    )
+    for src, dst in (
+        (inc.at[0], n_inc0), (inc.at[1], n_inc1), (prec.at[1], n_p1), (cr, n_cr), (cc, n_cc)
+    ):
+        fill(src, dst)
     own_codes(codes, 1, n_c1, up, dn, 8)
     for j in range(NJ):
         halo(n_inc0, j, blk(up, 0, j), blk(dn, 0, j))
@@ -377,8 +387,6 @@
         halo(n_cr, j, blk(up, 16, j), blk(dn, 16, j))
         halo(n_cc, j, blk(up, 24, j), blk(dn, 24, j))
         halo(n_p1, j, pltpu.roll(blk(up, 24, j), 5, 0), pltpu.roll(blk(dn, 24, j), 3, 0))
-    for c in copies:
-        c.wait()
     wn = (n_cr, n_cc)
     inside = inside_rows()
     misfit_stage(n_inc0, n_inc1, n_c1, wn, ta, n_m1)
@@ -395,23 +403,16 @@
 
 
 def first_body(
-    inc, prec, cr, cc, codes, up, dn, bulk_o, bulk_e, cor_o, w1, image1, mis_in,
+    prec, codes, up, dn, bulk_o, bulk_e, cor_o, w1, image1, n_inc0, n_inc1, n_cr, n_cc, mis_in,
     mis, adj,
-    n_prev, n_inc0, n_inc1, n_next, n_p0, n_pn, n_cr, n_cc, n_c0, n_cn, n_m0, n_a0, n_a1,
-    ta, tb, tw, isem, osem,
+    n_prev, n_next, n_p0, n_pn, n_c0, n_cn, n_m0, n_a0, n_a1, ta, tb, tw, osem,
 ):
     del mis_in
     even = parity() == 0
     cor_e = bulk_e.at[136:160]
-    copies = fetch(
-        [(inc.at[0], n_inc0), (inc.at[1], n_inc1), (prec.at[0], n_p0), (cr, n_cr), (cc, n_cc)], isem
-    )
+    fill(prec.at[0], n_p0)
     own_codes(codes, 0, n_c0, up, dn, 0)
     for j in range(NJ):
-        halo(n_inc0, j, blk(up, 0, j), blk(dn, 0, j))
-        halo(n_inc1, j, blk(up, 8, j), blk(dn, 8, j))
-        halo(n_cr, j, blk(up, 16, j), blk(dn, 16, j))
-        halo(n_cc, j, blk(up, 24, j), blk(dn, 24, j))
         halo(n_p0, j, pltpu.roll(blk(up, 16, j), 5, 0), pltpu.roll(blk(dn, 16, j), 3, 0))
 
     def previous(bulk, cor):
@@ -441,8 +442,6 @@
         previous(bulk_e, cor_e)
         following(bulk_o, cor_o)
 
-    for c in copies:
-        c.wait()
     wn = (n_cr, n_cc)
     inside = inside_rows()
     misfit_stage(n_prev, n_inc0, n_c0, wn, ta, n_m0)
@@ -471,14 +470,13 @@
 
 def last_step(*args):
     t = jax.ShapeDtypeStruct((F, NJ, 8, L), jnp.float32)
+    n = jax.ShapeDtypeStruct((NJ, 80, L), jnp.float32)
     return pl.pallas_call(
         last_body,
-        in_specs=[ON_HBM] * 4 + [ON_VMEM] * 3,
-        out_specs=[ON_HBM] + [ON_VMEM] * 2,
-        out_shape=[OUT, t, t],
-        scratch_shapes=[NAT] * 7
-        + [TFORM] * 3
-        + [pltpu.SemaphoreType.DMA((5 * NJ,)), pltpu.SemaphoreType.DMA((NJ,))],
+        in_specs=[ON_VMEM] * 7,
+        out_specs=[ON_HBM] + [ON_VMEM] * 6,
+        out_shape=[OUT, t, t, n, n, n, n],
+        scratch_shapes=[NAT] * 3 + [TFORM] * 3 + [pltpu.SemaphoreType.DMA((NJ,))],
         compiler_params=pltpu.CompilerParams(vmem_limit_bytes=24 << 20),
         name="last",
     )(*args)
@@ -487,13 +485,11 @@
 def first_steps(*args):
     return pl.pallas_call(
         first_body,
-        in_specs=[ON_HBM] * 4 + [ON_VMEM] * 8 + [ON_HBM],
+        in_specs=[ON_VMEM] * 13 + [ON_HBM],
         out_specs=[ON_HBM] * 2,
         out_shape=[OUT, OUT],
-        scratch_shapes=[NAT] * 13
-        + [TFORM] * 3
-        + [pltpu.SemaphoreType.DMA((5 * NJ,)), pltpu.SemaphoreType.DMA((3 * NJ,))],
-        input_output_aliases={12: 0},
+        scratch_shapes=[NAT] * 9 + [TFORM] * 3 + [pltpu.SemaphoreType.DMA((3 * NJ,))],
+        input_output_aliases={13: 0},
         compiler_params=pltpu.CompilerParams(vmem_limit_bytes=24 << 20),
         name="first",
     )(*args)
@@ -519,20 +515,24 @@
     return (t + 1 if t % 2 == 0 else t - 1), s
 
 
+def up_on_even(t, s):
+    return t, (s + 1 if t % 2 == 0 else s - 1)
+
+
+def down_on_even(t, s):
+    return t, (s - 1 if t % 2 == 0 else s + 1)
+
+
 def on_device(inc, prec, cr, cc, codes):
-    bulk_o, bulk_e, up, dn = pack(inc, prec, cr, cc, codes)
-    up = permute(up, lambda t, s: (t, s + 1))
+    bulk_o, bulk_e, pass_1, pass_2 = pack(inc, prec, cr, cc, codes)
     bulk_o = permute(bulk_o, off_chip)
-    dn = permute(dn, lambda t, s: (t, s - 1))
-    cor_o, bulk_e = corner(up, dn, bulk_e)
+    pass_1 = permute(pass_1, up_on_even)
+    pass_2 = permute(pass_2, down_on_even)
+    up, dn, cor_o, bulk_e = corner(pass_1, pass_2, bulk_e)
     cor_o = permute(cor_o, off_chip)
     bulk_e = permute(bulk_e, on_chip)
-    mis, w1, image1 = last_step(inc, prec, cr, cc, codes, up, dn)
-    return tuple(
-        first_steps(
-            inc, prec, cr, cc, codes, up, dn, bulk_o, bulk_e, cor_o, w1, image1, mis
-        )
-    )
+    mis, *kept = last_step(inc, prec, cr, cc, codes, up, dn)
+    return tuple(first_steps(prec, codes, up, dn, bulk_o, bulk_e, cor_o, *kept, mis))
 
 
 def solution(mesh):

time: 54.8 us -> 54.5 us (level)
  the two profiles are of different devices: /device:TPU:59 before, /device:TPU:6 now
where the time goes in v3:
time: 54.5 us; the launch traced here: 54.3 us
  starting transfers between devices  27.2 us (50%)
  waiting for transfers between devices  13.4 us (25%)
  Pallas kernels  12.9 us (24%)
  between operations  0.77 us (1%)
    ppermute x5, starting transfers between devices, permute(): return lax.ppermute(x, axes, pairs)  27.2 us
    ppermute x5, waiting for transfers between devices, permute(): return lax.ppermute(x, axes, pairs)  13.4 us
    pallas_call x1, Pallas kernels, first_steps(): pl.pallas_call(first_body, in_specs=[ON_VMEM] * 13 + [ON_HBM], out_specs=...  6.92 us
    pallas_call x1, Pallas kernels, last_step(): pl.pallas_call(last_body, in_specs=[ON_VMEM] * 7, out_specs=[ON_HBM] + [O...  3.79 us
    pallas_call x1, Pallas kernels, pack(): pl.pallas_call(pack_body, in_specs=[any_spec] * 5, out_specs=[vmem] * 4,...  2.14 us
  transfers between devices with their start and end apart: 5, of which 3 were waited for; matrix products, arithmetic and copies ran while one was open for 0% of the time, Pallas kernels for 7%

profile of v3, /device:TPU:6, one launch (start us, length us, event | category | flops | bytes accessed | tf_op | source)
XLA Modules:
  0.0 54.3 jit_solution(8322692759287032444)
XLA Ops:
  0.6 0.0 copy-start.1
  0.6 0.0 copy-start.3
  0.6 2.1 %pack.1 = (f32[136,2048]{1,0:T(8,128)S(1)}, f32[160,2048]{1,0:T(8,128)S(1)}, f32[32,2048]{1,0:T(8,128)S(1)}, f32[32,2048]{1,0:T(8,128)S(1)}) custom-call(f32[2,64,2048]{2,1,0:T(8,128)} %inc.3, f32[2,64,2048]{2,1,0:T(8,128)} %prec.5, f32[64,2048]{1,0:T(8,128)} %cr.3, f32[64,2048]{1,0:T(8,128)} %cc.3, s32[2,8,16]{2,1,0:T(8,128)} %codes.3), custom_call_target="tpu_custom_call" | custom-call | tf_op jit(solution)/shard_map/pack/pallas_call | solution.py:257
  2.8 0.0 copy-start
  2.8 0.0 copy-start.2
  2.8 0.0 copy-start.4
  2.8 4.4 %collective-permute-start = (f32[32,2048]{1,0:T(8,128)S(1)}, f32[32,2048]{1,0:T(8,128)S(1)}, u32[]{:S(2)}, u32[]{:S(2)}) collective-permute-start(f32[32,2048]{1,0:T(8,128)S(1)} %get-tuple-element.17), channel_id=1, source_target_pairs={{0,1},{1,2},{2,3},{3,4},{4,5},{5,6},{6,7},{7,8},{8,9},{9,10},{10,1... | collective-permute-start | bytes 786440 | tf_op jit(solution)/shard_map/ppermute | solution.py:507
  7.3 8.9 %collective-permute-start.1 = (f32[32,2048]{1,0:T(8,128)S(1)}, f32[32,2048]{1,0:T(8,128)S(1)}, u32[]{:S(2)}, u32[]{:S(2)}) collective-permute-start(f32[32,2048]{1,0:T(8,128)S(1)} %get-tuple-element.18), channel_id=1, source_target_pairs={{1,0},{2,1},{3,2},{4,3},{5,4},{6,5},{7,6},{8,7},{9,8},{10,9},{11,1... | collective-permute-start | bytes 786440 | tf_op jit(solution)/shard_map/ppermute | solution.py:507
  16.1 2.4 %collective-permute-done.pass_1 = f32[32,2048]{1,0:T(8,128)S(1)} collective-permute-done((f32[32,2048]{1,0:T(8,128)S(1)}, f32[32,2048]{1,0:T(8,128)S(1)}, u32[]{:S(2)}, u32[]{:S(2)}) %collective-permute-start) | collective-permute-done | bytes 262176 | tf_op jit(solution)/shard_map/ppermute | solution.py:507
  18.5 1.5 %collective-permute-done.1.pass_2 = f32[32,2048]{1,0:T(8,128)S(1)} collective-permute-done((f32[32,2048]{1,0:T(8,128)S(1)}, f32[32,2048]{1,0:T(8,128)S(1)}, u32[]{:S(2)}, u32[]{:S(2)}) %collective-permute-start.1) | collective-permute-done | bytes 262176 | tf_op jit(solution)/shard_map/ppermute | solution.py:507
  20.0 0.1 corner.1
  20.1 4.8 %collective-permute-start.3 = (f32[160,2048]{1,0:T(8,128)S(1)}, f32[160,2048]{1,0:T(8,128)S(1)}, u32[]{:S(2)}, u32[]{:S(2)}) collective-permute-start(f32[160,2048]{1,0:T(8,128)S(1)} %get-tuple-element.23), channel_id=1, source_target_pairs={{0,16},{1,17},{2,18},{3,19},{4,20},{5,21},{6,22},{7,23},{8,24},{9,... | collective-permute-start | bytes 3932168 | tf_op jit(solution)/shard_map/ppermute | solution.py:507
  24.8 5.5 %collective-permute-start.2 = (f32[136,2048]{1,0:T(8,128)S(1)}, f32[136,2048]{1,0:T(8,128)S(1)}, u32[]{:S(2)}, u32[]{:S(2)}) collective-permute-start(f32[136,2048]{1,0:T(8,128)S(1)} %get-tuple-element.22), channel_id=1, source_target_pairs={{16,32},{17,33},{18,34},{19,35},{20,36},{21,37},{22,38},{23,39},{2... | collective-permute-start | bytes 3342344 | tf_op jit(solution)/shard_map/ppermute | solution.py:507
  30.4 3.6 %collective-permute-start.4 = (f32[24,2048]{1,0:T(8,128)S(1)}, f32[24,2048]{1,0:T(8,128)S(1)}, u32[]{:S(2)}, u32[]{:S(2)}) collective-permute-start(f32[24,2048]{1,0:T(8,128)S(1)} %get-tuple-element.24), channel_id=1, source_target_pairs={{16,32},{17,33},{18,34},{19,35},{20,36},{21,37},{22,38},{23,39},{2... | collective-permute-start | bytes 589832 | tf_op jit(solution)/shard_map/ppermute | solution.py:507
  34.0 0.0 copy-done.1
  34.0 0.0 copy-done.3
  34.0 0.0 copy-done
  34.1 0.0 copy-done.2
  34.1 0.0 copy-done.4
  34.1 3.8 %last.1 = (f32[2,64,2048]{2,1,0:T(8,128)}, f32[10,16,8,128]{3,2,1,0:T(8,128)S(1)}, f32[10,16,8,128]{3,2,1,0:T(8,128)S(1)}, f32[16,80,128]{2,1,0:T(8,128)S(1)}, f...) custom-call(f32[2,64,2048]{2,1,0:T(8,128)S(1)} %copy-done.1, ...), custom_call_target="tpu_custom_call" | custom-call | tf_op jit(solution)/shard_map/last/pallas_call | solution.py:474
  37.9 9.5 %collective-permute-done.4.cor_o = f32[24,2048]{1,0:T(8,128)S(1)} collective-permute-done((f32[24,2048]{1,0:T(8,128)S(1)}, f32[24,2048]{1,0:T(8,128)S(1)}, u32[]{:S(2)}, u32[]{:S(2)}) %collective-permute-start.4) | collective-permute-done | bytes 196640 | tf_op jit(solution)/shard_map/ppermute | solution.py:507
  47.4 0.0 collective-permute-done.2.bulk_o
  47.4 0.0 collective-permute-done.3.bulk_e
  47.4 6.9 %first.1 = (f32[2,64,2048]{2,1,0:T(8,128)}, f32[2,64,2048]{2,1,0:T(8,128)}) custom-call(f32[2,64,2048]{2,1,0:T(8,128)S(1)} %copy-done, s32[2,8,16]{2,1,0:T(8,128)S(1)} %copy-done.4, f32[32,2048]{1,0:T(8,128)S(1)} %get-tuple-element.20.up, f32[32,2048]{1,0:T(8,128)S(1)} %get-tuple-element.21.dn, ...), custom_call_target="tpu_custom_call", output_to_operand_aliasing={{0}: (13, {})} | custom-call | tf_op jit(solution)/shard_map/first/pallas_call | solution.py:486
Async XLA Ops:
  0.6 33.4 %copy-start.1 = (f32[2,64,2048]{2,1,0:T(8,128)S(1)}, f32[2,64,2048]{2,1,0:T(8,128)}, u32[]{:S(2)}) copy-start(f32[2,64,2048]{2,1,0:T(8,128)} %inc.3) | copy-start | bytes 3145732
  0.6 33.4 %copy-start.3 = (f32[64,2048]{1,0:T(8,128)S(1)}, f32[64,2048]{1,0:T(8,128)}, u32[]{:S(2)}) copy-start(f32[64,2048]{1,0:T(8,128)} %cc.3) | copy-start | bytes 1572868
  2.8 31.2 %copy-start = (f32[2,64,2048]{2,1,0:T(8,128)S(1)}, f32[2,64,2048]{2,1,0:T(8,128)}, u32[]{:S(2)}) copy-start(f32[2,64,2048]{2,1,0:T(8,128)} %prec.5) | copy-start | bytes 3145732
  2.8 31.2 %copy-start.2 = (f32[64,2048]{1,0:T(8,128)S(1)}, f32[64,2048]{1,0:T(8,128)}, u32[]{:S(2)}) copy-start(f32[64,2048]{1,0:T(8,128)} %cr.3) | copy-start | bytes 1572868
  2.8 31.2 %copy-start.4 = (s32[2,8,16]{2,1,0:T(8,128)S(1)}, s32[2,8,16]{2,1,0:T(8,128)}, u32[]{:S(2)}) copy-start(s32[2,8,16]{2,1,0:T(8,128)} %codes.3) | copy-start | bytes 3076
  2.8 15.7 %collective-permute-start = (f32[32,2048]{1,0:T(8,128)S(1)}, f32[32,2048]{1,0:T(8,128)S(1)}, u32[]{:S(2)}, u32[]{:S(2)}) collective-permute-start(f32[32,2048]{1,0:T(8,128)S(1)} %get-tuple-element.17), channel_id=1, source_target_pairs={{0,1},{1,2},{2,3},{3,4},{4,5},{5,6},{6,7},{7,8},{8,9},{9,10},{10,1... | collective-permute-start | bytes 786440 | tf_op jit(solution)/shard_map/ppermute | solution.py:507
  7.3 12.7 %collective-permute-start.1 = (f32[32,2048]{1,0:T(8,128)S(1)}, f32[32,2048]{1,0:T(8,128)S(1)}, u32[]{:S(2)}, u32[]{:S(2)}) collective-permute-start(f32[32,2048]{1,0:T(8,128)S(1)} %get-tuple-element.18), channel_id=1, source_target_pairs={{1,0},{2,1},{3,2},{4,3},{5,4},{6,5},{7,6},{8,7},{9,8},{10,9},{11,1... | collective-permute-start | bytes 786440 | tf_op jit(solution)/shard_map/ppermute | solution.py:507
  20.1 27.3 %collective-permute-start.3 = (f32[160,2048]{1,0:T(8,128)S(1)}, f32[160,2048]{1,0:T(8,128)S(1)}, u32[]{:S(2)}, u32[]{:S(2)}) collective-permute-start(f32[160,2048]{1,0:T(8,128)S(1)} %get-tuple-element.23), channel_id=1, source_target_pairs={{0,16},{1,17},{2,18},{3,19},{4,20},{5,21},{6,22},{7,23},{8,24},{9,... | collective-permute-start | bytes 3932168 | tf_op jit(solution)/shard_map/ppermute | solution.py:507
  24.8 22.5 %collective-permute-start.2 = (f32[136,2048]{1,0:T(8,128)S(1)}, f32[136,2048]{1,0:T(8,128)S(1)}, u32[]{:S(2)}, u32[]{:S(2)}) collective-permute-start(f32[136,2048]{1,0:T(8,128)S(1)} %get-tuple-element.22), channel_id=1, source_target_pairs={{16,32},{17,33},{18,34},{19,35},{20,36},{21,37},{22,38},{23,39},{2... | collective-permute-start | bytes 3342344 | tf_op jit(solution)/shard_map/ppermute | solution.py:507
  30.4 17.0 %collective-permute-start.4 = (f32[24,2048]{1,0:T(8,128)S(1)}, f32[24,2048]{1,0:T(8,128)S(1)}, u32[]{:S(2)}, u32[]{:S(2)}) collective-permute-start(f32[24,2048]{1,0:T(8,128)S(1)} %get-tuple-element.24), channel_id=1, source_target_pairs={{16,32},{17,33},{18,34},{19,35},{20,36},{21,37},{22,38},{23,39},{2... | collective-permute-start | bytes 589832 | tf_op jit(solution)/shard_map/ppermute | solution.py:507

commit v4 on v3

--- a/solution.py
+++ b/solution.py
@@ -41,16 +41,6 @@
     return parts[0] if len(parts) == 1 else jnp.concatenate(parts, axis=0)
 
 
-def beside(u):
-    first = lanes() == 0
-    last = lanes() == L - 1
-    right_of = pltpu.roll(u[: G + 1], 1, 2)
-    left_of = pltpu.roll(u[1:], L - 1, 2)
-    left = jnp.where(first, right_of[:G], right_of[1:])
-    right = jnp.where(last, left_of[1:], left_of[:G])
-    return left, right
-
-
 def masks(code):
     mc = code < 1.5
     mr = jnp.where(mc, code, code - 2.0) < 0.5
@@ -58,28 +48,37 @@
 
 
 def stencil(get, visit):
-    for j0 in range(0, NJ, G):
-        above = pltpu.roll(get(F - 1, j0, G), 1, 1)
-        wide = get(0, j0 - 1, G + 2)
-        for f in range(F):
-            if f < F - 1:
-                after = get(f + 1, j0 - 1, G + 2)
-                below = after[1 : G + 1]
+    first = lanes() == 0
+    last = lanes() == L - 1
+    for f in range(F):
+        before = pltpu.roll(get(f, NJ - 1, 1), 1, 2)
+        here = get(f, 0, G)
+        back = pltpu.roll(here, L - 1, 2)
+        start = back[:1]
+        for j0 in range(0, NJ, G):
+            if j0 + G < NJ:
+                there = get(f, j0 + G, G)
+                back_there = pltpu.roll(there, L - 1, 2)
+                edge = back_there[:1]
             else:
-                after = None
-                below = pltpu.roll(get(0, j0, G), 7, 1)
-            visit(f, j0, wide, above, below)
-            above = wide[1 : G + 1]
-            wide = after
+                there = back_there = None
+                edge = start
+            fore = pltpu.roll(here, 1, 2)
+            left = jnp.where(first, jnp.concatenate([before, fore[: G - 1]], axis=0), fore)
+            right = jnp.where(last, jnp.concatenate([back[1:], edge], axis=0), back)
+            above = get(f - 1, j0, G) if f > 0 else pltpu.roll(get(F - 1, j0, G), 1, 1)
+            below = get(f + 1, j0, G) if f < F - 1 else pltpu.roll(get(0, j0, G), 7, 1)
+            visit(f, j0, here, left, right, above, below)
+            before = fore[G - 1 :]
+            here, back = there, back_there
 
 
 def misfit_stage(un, vn, code, wn, tout, out):
-    def visit(f, j0, u, up, down):
-        left, right = beside(u)
+    def visit(f, j0, u, left, right, up, down):
         mr, mc = masks(load(code, f, j0, G))
         cr, cc = load(wn[0], f, j0, G), load(wn[1], f, j0, G)
         moved = (
-            (1.0 - cr - cc) * u[1 : G + 1]
+            (1.0 - cr - cc) * u
             + cr * jnp.where(mr, up, down)
             + cc * jnp.where(mc, left, right)
         )
@@ -92,9 +91,8 @@
 
 
 def sweep_stage(tin, tout, after):
-    def visit(f, j0, u, up, down):
-        left, right = beside(u)
-        x = ((up + down) + (left + right)) + u[1 : G + 1]
+    def visit(f, j0, u, left, right, up, down):
+        x = ((up + down) + (left + right)) + u
         tout[f, j0 : j0 + G] = after(x, f, j0)
 
     stencil(lambda f, j0, n: load_t(tin, f, j0, n), visit)
@@ -219,13 +217,7 @@
             dn[16:24, cols] = jnp.where(row > 4, pltpu.roll(p0t, 5, 0), crt)
             dn[24:32, cols] = jnp.where(row > 4, pltpu.roll(p1t, 5, 0), cct)
 
-    @pl.when(even)
-    def _():
-        edges(pass_1, pass_2)
-
-    @pl.when(jnp.logical_not(even))
-    def _():
-        edges(pass_2, pass_1)
+    edges(pass_1, pass_2)
 
     @pl.when(even)
     def _():
@@ -298,7 +290,7 @@
 
     @pl.when(jnp.logical_not(even))
     def _():
-        both(pass_2, pass_1, cor_o, cor_e)
+        both(pass_1, pass_2, cor_o, cor_e)
 
 
 def corner(pass_1, pass_2, bulk_e):
@@ -516,11 +508,11 @@
 
 
 def up_on_even(t, s):
-    return t, (s + 1 if t % 2 == 0 else s - 1)
+    return t, s + 1
 
 
 def down_on_even(t, s):
-    return t, (s - 1 if t % 2 == 0 else s + 1)
+    return t, s - 1
 
 
 def on_device(inc, prec, cr, cc, codes):

time: 54.5 us -> 52.9 us (0.971)
  the two profiles are of different devices: /device:TPU:6 before, /device:TPU:59 now
where the time goes in v4:
time: 52.9 us; the launch traced here: 52.7 us
  starting transfers between devices  25.5 us (48%)
  waiting for transfers between devices  14.5 us (27%)
  Pallas kernels  11.9 us (22%)
  between operations  0.77 us (1%)
    ppermute x5, starting transfers between devices, permute(): return lax.ppermute(x, axes, pairs)  25.5 us
    ppermute x5, waiting for transfers between devices, permute(): return lax.ppermute(x, axes, pairs)  14.5 us
    pallas_call x1, Pallas kernels, first_steps(): pl.pallas_call(first_body, in_specs=[ON_VMEM] * 13 + [ON_HBM], out_specs=...  6.27 us
    pallas_call x1, Pallas kernels, last_step(): pl.pallas_call(last_body, in_specs=[ON_VMEM] * 7, out_specs=[ON_HBM] + [O...  3.57 us
    pallas_call x1, Pallas kernels, pack(): pl.pallas_call(pack_body, in_specs=[any_spec] * 5, out_specs=[vmem] * 4,...  1.98 us
  transfers between devices with their start and end apart: 5, of which 3 were waited for; matrix products, arithmetic and copies ran while one was open for 0% of the time, Pallas kernels for 7%

profile of v4, /device:TPU:59, one launch (start us, length us, event | category | flops | bytes accessed | tf_op | source)
XLA Modules:
  0.0 52.7 jit_solution(12324575053162363640)
XLA Ops:
  0.6 0.0 copy-start.1
  0.6 0.0 copy-start.3
  0.6 2.0 %pack.1 = (f32[136,2048]{1,0:T(8,128)S(1)}, f32[160,2048]{1,0:T(8,128)S(1)}, f32[32,2048]{1,0:T(8,128)S(1)}, f32[32,2048]{1,0:T(8,128)S(1)}) custom-call(f32[2,64,2048]{2,1,0:T(8,128)} %inc.3, f32[2,64,2048]{2,1,0:T(8,128)} %prec.5, f32[64,2048]{1,0:T(8,128)} %cr.3, f32[64,2048]{1,0:T(8,128)} %cc.3, s32[2,8,16]{2,1,0:T(8,128)} %codes.3), custom_call_target="tpu_custom_call" | custom-call | tf_op jit(solution)/shard_map/pack/pallas_call | solution.py:249
  2.6 0.0 copy-start
  2.7 0.0 copy-start.2
  2.7 0.0 copy-start.4
  2.7 4.1 %collective-permute-start = (f32[32,2048]{1,0:T(8,128)S(1)}, f32[32,2048]{1,0:T(8,128)S(1)}, u32[]{:S(2)}, u32[]{:S(2)}) collective-permute-start(f32[32,2048]{1,0:T(8,128)S(1)} %get-tuple-element.17), channel_id=1, source_target_pairs={{0,1},{1,2},{2,3},{3,4},{4,5},{5,6},{6,7},{7,8},{8,9},{9,10},{10,1... | collective-permute-start | bytes 786440 | tf_op jit(solution)/shard_map/ppermute | solution.py:499
  6.8 8.6 %collective-permute-start.1 = (f32[32,2048]{1,0:T(8,128)S(1)}, f32[32,2048]{1,0:T(8,128)S(1)}, u32[]{:S(2)}, u32[]{:S(2)}) collective-permute-start(f32[32,2048]{1,0:T(8,128)S(1)} %get-tuple-element.18), channel_id=1, source_target_pairs={{1,0},{2,1},{3,2},{4,3},{5,4},{6,5},{7,6},{8,7},{9,8},{10,9},{11,1... | collective-permute-start | bytes 786440 | tf_op jit(solution)/shard_map/ppermute | solution.py:499
  15.4 3.9 %collective-permute-done.pass_1 = f32[32,2048]{1,0:T(8,128)S(1)} collective-permute-done((f32[32,2048]{1,0:T(8,128)S(1)}, f32[32,2048]{1,0:T(8,128)S(1)}, u32[]{:S(2)}, u32[]{:S(2)}) %collective-permute-start) | collective-permute-done | bytes 262176 | tf_op jit(solution)/shard_map/ppermute | solution.py:499
  19.3 0.9 %collective-permute-done.1.pass_2 = f32[32,2048]{1,0:T(8,128)S(1)} collective-permute-done((f32[32,2048]{1,0:T(8,128)S(1)}, f32[32,2048]{1,0:T(8,128)S(1)}, u32[]{:S(2)}, u32[]{:S(2)}) %collective-permute-start.1) | collective-permute-done | bytes 262176 | tf_op jit(solution)/shard_map/ppermute | solution.py:499
  20.2 0.1 corner.1
  20.3 3.6 %collective-permute-start.3 = (f32[160,2048]{1,0:T(8,128)S(1)}, f32[160,2048]{1,0:T(8,128)S(1)}, u32[]{:S(2)}, u32[]{:S(2)}) collective-permute-start(f32[160,2048]{1,0:T(8,128)S(1)} %get-tuple-element.23), channel_id=1, source_target_pairs={{0,16},{1,17},{2,18},{3,19},{4,20},{5,21},{6,22},{7,23},{8,24},{9,... | collective-permute-start | bytes 3932168 | tf_op jit(solution)/shard_map/ppermute | solution.py:499
  23.9 3.1 %collective-permute-start.2 = (f32[136,2048]{1,0:T(8,128)S(1)}, f32[136,2048]{1,0:T(8,128)S(1)}, u32[]{:S(2)}, u32[]{:S(2)}) collective-permute-start(f32[136,2048]{1,0:T(8,128)S(1)} %get-tuple-element.22), channel_id=1, source_target_pairs={{16,32},{17,33},{18,34},{19,35},{20,36},{21,37},{22,38},{23,39},{2... | collective-permute-start | bytes 3342344 | tf_op jit(solution)/shard_map/ppermute | solution.py:499
  27.0 6.0 %collective-permute-start.4 = (f32[24,2048]{1,0:T(8,128)S(1)}, f32[24,2048]{1,0:T(8,128)S(1)}, u32[]{:S(2)}, u32[]{:S(2)}) collective-permute-start(f32[24,2048]{1,0:T(8,128)S(1)} %get-tuple-element.24), channel_id=1, source_target_pairs={{16,32},{17,33},{18,34},{19,35},{20,36},{21,37},{22,38},{23,39},{2... | collective-permute-start | bytes 589832 | tf_op jit(solution)/shard_map/ppermute | solution.py:499
  33.1 0.0 copy-done.1
  33.1 0.0 copy-done.3
  33.1 0.0 copy-done
  33.1 0.0 copy-done.2
  33.1 0.0 copy-done.4
  33.1 3.6 %last.1 = (f32[2,64,2048]{2,1,0:T(8,128)}, f32[10,16,8,128]{3,2,1,0:T(8,128)S(1)}, f32[10,16,8,128]{3,2,1,0:T(8,128)S(1)}, f32[16,80,128]{2,1,0:T(8,128)S(1)}, f...) custom-call(f32[2,64,2048]{2,1,0:T(8,128)S(1)} %copy-done.1, ...), custom_call_target="tpu_custom_call" | custom-call | tf_op jit(solution)/shard_map/last/pallas_call | solution.py:466
  36.7 9.7 %collective-permute-done.4.cor_o = f32[24,2048]{1,0:T(8,128)S(1)} collective-permute-done((f32[24,2048]{1,0:T(8,128)S(1)}, f32[24,2048]{1,0:T(8,128)S(1)}, u32[]{:S(2)}, u32[]{:S(2)}) %collective-permute-start.4) | collective-permute-done | bytes 196640 | tf_op jit(solution)/shard_map/ppermute | solution.py:499
  46.4 0.0 collective-permute-done.2.bulk_o
  46.4 0.0 collective-permute-done.3.bulk_e
  46.4 6.3 %first.1 = (f32[2,64,2048]{2,1,0:T(8,128)}, f32[2,64,2048]{2,1,0:T(8,128)}) custom-call(f32[2,64,2048]{2,1,0:T(8,128)S(1)} %copy-done, s32[2,8,16]{2,1,0:T(8,128)S(1)} %copy-done.4, f32[32,2048]{1,0:T(8,128)S(1)} %get-tuple-element.20.up, f32[32,2048]{1,0:T(8,128)S(1)} %get-tuple-element.21.dn, ...), custom_call_target="tpu_custom_call", output_to_operand_aliasing={{0}: (13, {})} | custom-call | tf_op jit(solution)/shard_map/first/pallas_call | solution.py:478
Async XLA Ops:
  0.6 32.4 %copy-start.1 = (f32[2,64,2048]{2,1,0:T(8,128)S(1)}, f32[2,64,2048]{2,1,0:T(8,128)}, u32[]{:S(2)}) copy-start(f32[2,64,2048]{2,1,0:T(8,128)} %inc.3) | copy-start | bytes 3145732
  0.6 32.4 %copy-start.3 = (f32[64,2048]{1,0:T(8,128)S(1)}, f32[64,2048]{1,0:T(8,128)}, u32[]{:S(2)}) copy-start(f32[64,2048]{1,0:T(8,128)} %cc.3) | copy-start | bytes 1572868
  2.6 30.4 %copy-start = (f32[2,64,2048]{2,1,0:T(8,128)S(1)}, f32[2,64,2048]{2,1,0:T(8,128)}, u32[]{:S(2)}) copy-start(f32[2,64,2048]{2,1,0:T(8,128)} %prec.5) | copy-start | bytes 3145732
  2.7 30.4 %copy-start.2 = (f32[64,2048]{1,0:T(8,128)S(1)}, f32[64,2048]{1,0:T(8,128)}, u32[]{:S(2)}) copy-start(f32[64,2048]{1,0:T(8,128)} %cr.3) | copy-start | bytes 1572868
  2.7 30.4 %copy-start.4 = (s32[2,8,16]{2,1,0:T(8,128)S(1)}, s32[2,8,16]{2,1,0:T(8,128)}, u32[]{:S(2)}) copy-start(s32[2,8,16]{2,1,0:T(8,128)} %codes.3) | copy-start | bytes 3076
  2.7 16.6 %collective-permute-start = (f32[32,2048]{1,0:T(8,128)S(1)}, f32[32,2048]{1,0:T(8,128)S(1)}, u32[]{:S(2)}, u32[]{:S(2)}) collective-permute-start(f32[32,2048]{1,0:T(8,128)S(1)} %get-tuple-element.17), channel_id=1, source_target_pairs={{0,1},{1,2},{2,3},{3,4},{4,5},{5,6},{6,7},{7,8},{8,9},{9,10},{10,1... | collective-permute-start | bytes 786440 | tf_op jit(solution)/shard_map/ppermute | solution.py:499
  6.8 13.4 %collective-permute-start.1 = (f32[32,2048]{1,0:T(8,128)S(1)}, f32[32,2048]{1,0:T(8,128)S(1)}, u32[]{:S(2)}, u32[]{:S(2)}) collective-permute-start(f32[32,2048]{1,0:T(8,128)S(1)} %get-tuple-element.18), channel_id=1, source_target_pairs={{1,0},{2,1},{3,2},{4,3},{5,4},{6,5},{7,6},{8,7},{9,8},{10,9},{11,1... | collective-permute-start | bytes 786440 | tf_op jit(solution)/shard_map/ppermute | solution.py:499
  20.3 26.2 %collective-permute-start.3 = (f32[160,2048]{1,0:T(8,128)S(1)}, f32[160,2048]{1,0:T(8,128)S(1)}, u32[]{:S(2)}, u32[]{:S(2)}) collective-permute-start(f32[160,2048]{1,0:T(8,128)S(1)} %get-tuple-element.23), channel_id=1, source_target_pairs={{0,16},{1,17},{2,18},{3,19},{4,20},{5,21},{6,22},{7,23},{8,24},{9,... | collective-permute-start | bytes 3932168 | tf_op jit(solution)/shard_map/ppermute | solution.py:499
  23.9 22.5 %collective-permute-start.2 = (f32[136,2048]{1,0:T(8,128)S(1)}, f32[136,2048]{1,0:T(8,128)S(1)}, u32[]{:S(2)}, u32[]{:S(2)}) collective-permute-start(f32[136,2048]{1,0:T(8,128)S(1)} %get-tuple-element.22), channel_id=1, source_target_pairs={{16,32},{17,33},{18,34},{19,35},{20,36},{21,37},{22,38},{23,39},{2... | collective-permute-start | bytes 3342344 | tf_op jit(solution)/shard_map/ppermute | solution.py:499
  27.0 19.4 %collective-permute-start.4 = (f32[24,2048]{1,0:T(8,128)S(1)}, f32[24,2048]{1,0:T(8,128)S(1)}, u32[]{:S(2)}, u32[]{:S(2)}) collective-permute-start(f32[24,2048]{1,0:T(8,128)S(1)} %get-tuple-element.24), channel_id=1, source_target_pairs={{16,32},{17,33},{18,34},{19,35},{20,36},{21,37},{22,38},{23,39},{2... | collective-permute-start | bytes 589832 | tf_op jit(solution)/shard_map/ppermute | solution.py:499

commit v5 on v4

--- a/solution.py
+++ b/solution.py
@@ -111,7 +111,7 @@
     sweep_stage(tmp, tout, lambda x, f, j0: x)
 
 
-def adjoint_stage(tw, code, wn, emit):
+def adjoint_stage(tw, code, wn, emit, done=lambda j0: None):
     first = lanes() == 0
     last = lanes() == L - 1
 
@@ -153,6 +153,7 @@
             above = upper
             if after is not None:
                 image, lower, upper = after
+        done(j0)
 
 
 def parity():
@@ -326,12 +327,12 @@
             dst[j, 8 + 8 * b : 16 + 8 * b] = src[8 * b : 8 * b + 8, j * L : (j + 1) * L]
 
 
-def emit_out(nat, dst, sem, base):
+def emit_out(nat, dst, sem, base, blocks=range(NJ)):
     copies = [
         pltpu.make_async_copy(
             nat.at[j, pl.ds(8, 64)], dst.at[:, pl.ds(j * L, L)], sem.at[base + j]
         )
-        for j in range(NJ)
+        for j in blocks
     ]
     for c in copies:
         c.start()
@@ -355,24 +356,38 @@
     return inside
 
 
-def own_codes(codes, step, n_c, up, dn, r):
+def own_codes(codes, step, n_c):
     rows = code_rows(codes, step)
     for j in range(NJ):
         for b in range(8):
             spread(n_c, j, 8 + 8 * b, rows[j][b : b + 1])
+
+
+def halo_codes(n_c, up, dn, r):
+    for j in range(NJ):
         spread(n_c, j, 0, blk(up, r, j)[0:1])
         spread(n_c, j, 72, blk(dn, r, j)[7:8])
 
 
-def last_body(
-    inc, prec, cr, cc, codes, up, dn, mis, w_out, image_out, n_inc0, n_inc1, n_cr, n_cc,
-    n_p1, n_c1, n_m1, ta, tb, tw, osem,
+def prepare_body(
+    inc, prec, cr, cc, codes, n_inc0, n_inc1, n_cr, n_cc, n_p0, n_p1, n_c0, n_c1
 ):
     for src, dst in (
-        (inc.at[0], n_inc0), (inc.at[1], n_inc1), (prec.at[1], n_p1), (cr, n_cr), (cc, n_cc)
+        (inc.at[0], n_inc0), (inc.at[1], n_inc1), (cr, n_cr), (cc, n_cc),
+        (prec.at[0], n_p0), (prec.at[1], n_p1),
     ):
         fill(src, dst)
-    own_codes(codes, 1, n_c1, up, dn, 8)
+    own_codes(codes, 0, n_c0)
+    own_codes(codes, 1, n_c1)
+
+
+def last_body(
+    up, dn, in_inc0, in_inc1, in_cr, in_cc, in_p1, in_c1,
+    mis, w_out, image_out, n_inc0, n_inc1, n_cr, n_cc, n_p1, n_c1,
+    n_m1, ta, tb, tw, osem,
+):
+    del in_inc0, in_inc1, in_cr, in_cc, in_p1, in_c1
+    halo_codes(n_c1, up, dn, 8)
     for j in range(NJ):
         halo(n_inc0, j, blk(up, 0, j), blk(dn, 0, j))
         halo(n_inc1, j, blk(up, 8, j), blk(dn, 8, j))
@@ -395,15 +410,14 @@
 
 
 def first_body(
-    prec, codes, up, dn, bulk_o, bulk_e, cor_o, w1, image1, n_inc0, n_inc1, n_cr, n_cc, mis_in,
-    mis, adj,
-    n_prev, n_next, n_p0, n_pn, n_c0, n_cn, n_m0, n_a0, n_a1, ta, tb, tw, osem,
+    up, dn, bulk_o, bulk_e, cor_o, w1, image1, n_inc0, n_inc1, n_cr, n_cc, in_p0, in_c0, mis_in,
+    mis, adj, n_p0, n_c0,
+    n_prev, n_next, n_pn, n_cn, n_m0, n_a0, n_a1, ta, tb, tw, osem,
 ):
-    del mis_in
+    del in_p0, in_c0, mis_in
     even = parity() == 0
     cor_e = bulk_e.at[136:160]
-    fill(prec.at[0], n_p0)
-    own_codes(codes, 0, n_c0, up, dn, 0)
+    halo_codes(n_c0, up, dn, 0)
     for j in range(NJ):
         halo(n_p0, j, pltpu.roll(blk(up, 16, j), 5, 0), pltpu.roll(blk(dn, 16, j), 3, 0))
 
@@ -446,9 +460,12 @@
     misfit_stage(n_inc1, n_next, n_cn, wn, ta, None)
     smooth_stages(ta, tb, n_pn, tw, inside)
     adjoint_stage(
-        tw, n_cn, wn, lambda f, j0, image: save(n_a1, f, j0, w1[f, j0 : j0 + G] - image)
+        tw,
+        n_cn,
+        wn,
+        lambda f, j0, image: save(n_a1, f, j0, w1[f, j0 : j0 + G] - image),
+        lambda j0: outs.extend(emit_out(n_a1, adj.at[1], osem, 2 * NJ, range(j0, j0 + G))),
     )
-    outs += emit_out(n_a1, adj.at[1], osem, 2 * NJ)
     for c in outs:
         c.wait()
 
@@ -460,15 +477,29 @@
 OUT = jax.ShapeDtypeStruct((2, 64, 2048), jnp.float32)
 
 
+NAT_OUT = jax.ShapeDtypeStruct((NJ, 80, L), jnp.float32)
+T_OUT = jax.ShapeDtypeStruct((F, NJ, 8, L), jnp.float32)
+
+
+def prepare(*args):
+    return pl.pallas_call(
+        prepare_body,
+        in_specs=[ON_VMEM] * 5,
+        out_specs=[ON_VMEM] * 8,
+        out_shape=[NAT_OUT] * 8,
+        compiler_params=pltpu.CompilerParams(vmem_limit_bytes=16 << 20),
+        name="prepare",
+    )(*args)
+
+
 def last_step(*args):
-    t = jax.ShapeDtypeStruct((F, NJ, 8, L), jnp.float32)
-    n = jax.ShapeDtypeStruct((NJ, 80, L), jnp.float32)
     return pl.pallas_call(
         last_body,
-        in_specs=[ON_VMEM] * 7,
-        out_specs=[ON_HBM] + [ON_VMEM] * 6,
-        out_shape=[OUT, t, t, n, n, n, n],
-        scratch_shapes=[NAT] * 3 + [TFORM] * 3 + [pltpu.SemaphoreType.DMA((NJ,))],
+        in_specs=[ON_VMEM] * 8,
+        out_specs=[ON_HBM] + [ON_VMEM] * 8,
+        out_shape=[OUT, T_OUT, T_OUT] + [NAT_OUT] * 6,
+        scratch_shapes=[NAT] + [TFORM] * 3 + [pltpu.SemaphoreType.DMA((NJ,))],
+        input_output_aliases={2 + k: 3 + k for k in range(6)},
         compiler_params=pltpu.CompilerParams(vmem_limit_bytes=24 << 20),
         name="last",
     )(*args)
@@ -478,10 +509,10 @@
     return pl.pallas_call(
         first_body,
         in_specs=[ON_VMEM] * 13 + [ON_HBM],
-        out_specs=[ON_HBM] * 2,
-        out_shape=[OUT, OUT],
-        scratch_shapes=[NAT] * 9 + [TFORM] * 3 + [pltpu.SemaphoreType.DMA((3 * NJ,))],
-        input_output_aliases={13: 0},
+        out_specs=[ON_HBM] * 2 + [ON_VMEM] * 2,
+        out_shape=[OUT, OUT, NAT_OUT, NAT_OUT],
+        scratch_shapes=[NAT] * 7 + [TFORM] * 3 + [pltpu.SemaphoreType.DMA((3 * NJ,))],
+        input_output_aliases={13: 0, 11: 2, 12: 3},
         compiler_params=pltpu.CompilerParams(vmem_limit_bytes=24 << 20),
         name="first",
     )(*args)
@@ -523,8 +554,10 @@
     up, dn, cor_o, bulk_e = corner(pass_1, pass_2, bulk_e)
     cor_o = permute(cor_o, off_chip)
     bulk_e = permute(bulk_e, on_chip)
-    mis, *kept = last_step(inc, prec, cr, cc, codes, up, dn)
-    return tuple(first_steps(prec, codes, up, dn, bulk_o, bulk_e, cor_o, *kept, mis))
+    inc0, inc1, cr, cc, p0, p1, c0, c1 = prepare(inc, prec, cr, cc, codes)
+    mis, w1, image1, inc0, inc1, cr, cc, _, _ = last_step(up, dn, inc0, inc1, cr, cc, p1, c1)
+    outs = first_steps(up, dn, bulk_o, bulk_e, cor_o, w1, image1, inc0, inc1, cr, cc, p0, c0, mis)
+    return outs[0], outs[1]
 
 
 def solution(mesh):

time: 52.9 us -> 52.2 us (0.987)
    pallas_call x1, Pallas kernels: 6.27 us -> 5.61 us  [first_steps(): pl.pallas_call(first_body, in_specs=[ON_VMEM] * 13 + [ON_HBM], out_specs=...]
    pallas_call x1 -> x2, Pallas kernels: 3.57 us -> 3.73 us  [the longest x1 3.21 us: last_step(): pl.pallas_call(last_body, in_specs=[ON_VMEM] * 8, out_specs=[ON_HBM] + [O...]
where the time goes in v5:
time: 52.2 us; the launch traced here: 52 us
  starting transfers between devices  25.5 us (49%)
  waiting for transfers between devices  14.4 us (28%)
  Pallas kernels  11.4 us (22%)
  between operations  0.78 us (1%)
    ppermute x5, starting transfers between devices, permute(): return lax.ppermute(x, axes, pairs)  25.5 us
    ppermute x5, waiting for transfers between devices, permute(): return lax.ppermute(x, axes, pairs)  14.4 us
    pallas_call x1, Pallas kernels, first_steps(): pl.pallas_call(first_body, in_specs=[ON_VMEM] * 13 + [ON_HBM], out_specs=...  5.61 us
    pallas_call x1, Pallas kernels, last_step(): pl.pallas_call(last_body, in_specs=[ON_VMEM] * 8, out_specs=[ON_HBM] + [O...  3.21 us
    pallas_call x1, Pallas kernels, pack(): pl.pallas_call(pack_body, in_specs=[any_spec] * 5, out_specs=[vmem] * 4,...  1.98 us
  transfers between devices with their start and end apart: 5, of which 3 were waited for; matrix products, arithmetic and copies ran while one was open for 0% of the time, Pallas kernels for 7%

profile of v5, /device:TPU:59, one launch (start us, length us, event | category | flops | bytes accessed | tf_op | source)
XLA Modules:
  0.0 52.0 jit_solution(15401739738220583405)
XLA Ops:
  0.6 0.0 copy-start.1
  0.6 0.0 copy-start.3
  0.6 2.0 %pack.1 = (f32[136,2048]{1,0:T(8,128)S(1)}, f32[160,2048]{1,0:T(8,128)S(1)}, f32[32,2048]{1,0:T(8,128)S(1)}, f32[32,2048]{1,0:T(8,128)S(1)}) custom-call(f32[2,64,2048]{2,1,0:T(8,128)} %inc.3, f32[2,64,2048]{2,1,0:T(8,128)} %prec.3, f32[64,2048]{1,0:T(8,128)} %cr.3, f32[64,2048]{1,0:T(8,128)} %cc.3, s32[2,8,16]{2,1,0:T(8,128)} %codes.1), custom_call_target="tpu_custom_call" | custom-call | tf_op jit(solution)/shard_map/pack/pallas_call | solution.py:250
  2.6 0.0 copy-start
  2.7 0.0 copy-start.2
  2.7 0.0 copy-start.4
  2.7 4.1 %collective-permute-start = (f32[32,2048]{1,0:T(8,128)S(1)}, f32[32,2048]{1,0:T(8,128)S(1)}, u32[]{:S(2)}, u32[]{:S(2)}) collective-permute-start(f32[32,2048]{1,0:T(8,128)S(1)} %get-tuple-element.27), channel_id=1, source_target_pairs={{0,1},{1,2},{2,3},{3,4},{4,5},{5,6},{6,7},{7,8},{8,9},{9,10},{10,1... | collective-permute-start | bytes 786440 | tf_op jit(solution)/shard_map/ppermute | solution.py:530
  6.8 8.6 %collective-permute-start.1 = (f32[32,2048]{1,0:T(8,128)S(1)}, f32[32,2048]{1,0:T(8,128)S(1)}, u32[]{:S(2)}, u32[]{:S(2)}) collective-permute-start(f32[32,2048]{1,0:T(8,128)S(1)} %get-tuple-element.28), channel_id=1, source_target_pairs={{1,0},{2,1},{3,2},{4,3},{5,4},{6,5},{7,6},{8,7},{9,8},{10,9},{11,1... | collective-permute-start | bytes 786440 | tf_op jit(solution)/shard_map/ppermute | solution.py:530
  15.4 3.9 %collective-permute-done.pass_1 = f32[32,2048]{1,0:T(8,128)S(1)} collective-permute-done((f32[32,2048]{1,0:T(8,128)S(1)}, f32[32,2048]{1,0:T(8,128)S(1)}, u32[]{:S(2)}, u32[]{:S(2)}) %collective-permute-start) | collective-permute-done | bytes 262176 | tf_op jit(solution)/shard_map/ppermute | solution.py:530
  19.3 0.9 %collective-permute-done.1.pass_2 = f32[32,2048]{1,0:T(8,128)S(1)} collective-permute-done((f32[32,2048]{1,0:T(8,128)S(1)}, f32[32,2048]{1,0:T(8,128)S(1)}, u32[]{:S(2)}, u32[]{:S(2)}) %collective-permute-start.1) | collective-permute-done | bytes 262176 | tf_op jit(solution)/shard_map/ppermute | solution.py:530
  20.2 0.1 corner.1
  20.3 3.6 %collective-permute-start.3 = (f32[160,2048]{1,0:T(8,128)S(1)}, f32[160,2048]{1,0:T(8,128)S(1)}, u32[]{:S(2)}, u32[]{:S(2)}) collective-permute-start(f32[160,2048]{1,0:T(8,128)S(1)} %get-tuple-element.33), channel_id=1, source_target_pairs={{0,16},{1,17},{2,18},{3,19},{4,20},{5,21},{6,22},{7,23},{8,24},{9,... | collective-permute-start | bytes 3932168 | tf_op jit(solution)/shard_map/ppermute | solution.py:530
  23.9 3.1 %collective-permute-start.2 = (f32[136,2048]{1,0:T(8,128)S(1)}, f32[136,2048]{1,0:T(8,128)S(1)}, u32[]{:S(2)}, u32[]{:S(2)}) collective-permute-start(f32[136,2048]{1,0:T(8,128)S(1)} %get-tuple-element.32), channel_id=1, source_target_pairs={{16,32},{17,33},{18,34},{19,35},{20,36},{21,37},{22,38},{23,39},{2... | collective-permute-start | bytes 3342344 | tf_op jit(solution)/shard_map/ppermute | solution.py:530
  27.0 6.0 %collective-permute-start.4 = (f32[24,2048]{1,0:T(8,128)S(1)}, f32[24,2048]{1,0:T(8,128)S(1)}, u32[]{:S(2)}, u32[]{:S(2)}) collective-permute-start(f32[24,2048]{1,0:T(8,128)S(1)} %get-tuple-element.34), channel_id=1, source_target_pairs={{16,32},{17,33},{18,34},{19,35},{20,36},{21,37},{22,38},{23,39},{2... | collective-permute-start | bytes 589832 | tf_op jit(solution)/shard_map/ppermute | solution.py:530
  33.1 0.0 copy-done.1
  33.1 0.0 copy-done.3
  33.1 0.0 copy-done
  33.1 0.0 copy-done.2
  33.1 0.0 copy-done.4
  33.1 0.5 %prepare.1 = (f32[16,80,128]{2,1,0:T(8,128)S(1)}, f32[16,80,128]{2,1,0:T(8,128)S(1)}, f32[16,80,128]{2,1,0:T(8,128)S(1)}, f32[16,80,128]{2,1,0:T(8,128)S(1)}, f3...) custom-call(f32[2,64,2048]{2,1,0:T(8,128)S(1)} %copy-done, ...), custom_call_target="tpu_custom_call" | custom-call | tf_op jit(solution)/shard_map/prepare/pallas_call | solution.py:485
  33.6 3.2 %last.1 = (f32[2,64,2048]{2,1,0:T(8,128)}, f32[10,16,8,128]{3,2,1,0:T(8,128)S(1)}, f32[10,16,8,128]{3,2,1,0:T(8,128)S(1)}, f32[16,80,128]{2,1,0:T(8,128)S(1)}, f...) custom-call(f32[32,2048]{1,0:T(8,128)S(1)} %get-tuple-element.30.up,, ...), custom_call_target="tpu_custom_call", output_to_operand_aliasing={{3}: (2, {}), {4}: (3, {}), {5}: (4, {}), {6}: (5, {}), {7}... | custom-call | tf_op jit(solution)/shard_map/last/pallas_call | solution.py:496
  36.9 9.5 %collective-permute-done.4.cor_o = f32[24,2048]{1,0:T(8,128)S(1)} collective-permute-done((f32[24,2048]{1,0:T(8,128)S(1)}, f32[24,2048]{1,0:T(8,128)S(1)}, u32[]{:S(2)}, u32[]{:S(2)}) %collective-permute-start.4) | collective-permute-done | bytes 196640 | tf_op jit(solution)/shard_map/ppermute | solution.py:530
  46.4 0.0 collective-permute-done.2.bulk_o
  46.4 0.0 collective-permute-done.3.bulk_e
  46.4 5.6 %first.1 = (f32[2,64,2048]{2,1,0:T(8,128)}, f32[2,64,2048]{2,1,0:T(8,128)}, f32[16,80,128]{2,1,0:T(8,128)S(1)}, f32[16,80,128]{2,1,0:T(8,128)S(1)}) custom-call(f32[32,2048]{1,0:T(8,128)S(1)} %get-tuple-element.30.up, f32[32,2048]{1,0:T(8,128)S(1)} %get-tuple-element.31.dn, ...), custom_call_target="tpu_custom_call", output_to_operand_aliasing={{0}: (13, {}), {2}: (11, {}), {3}: (12, {})} | custom-call | tf_op jit(solution)/shard_map/first/pallas_call | solution.py:509
Async XLA Ops:
  0.6 32.4 %copy-start.1 = (f32[2,64,2048]{2,1,0:T(8,128)S(1)}, f32[2,64,2048]{2,1,0:T(8,128)}, u32[]{:S(2)}) copy-start(f32[2,64,2048]{2,1,0:T(8,128)} %prec.3) | copy-start | bytes 3145732
  0.6 32.4 %copy-start.3 = (f32[64,2048]{1,0:T(8,128)S(1)}, f32[64,2048]{1,0:T(8,128)}, u32[]{:S(2)}) copy-start(f32[64,2048]{1,0:T(8,128)} %cc.3) | copy-start | bytes 1572868
  2.6 30.4 %copy-start = (f32[2,64,2048]{2,1,0:T(8,128)S(1)}, f32[2,64,2048]{2,1,0:T(8,128)}, u32[]{:S(2)}) copy-start(f32[2,64,2048]{2,1,0:T(8,128)} %inc.3) | copy-start | bytes 3145732
  2.7 30.4 %copy-start.2 = (f32[64,2048]{1,0:T(8,128)S(1)}, f32[64,2048]{1,0:T(8,128)}, u32[]{:S(2)}) copy-start(f32[64,2048]{1,0:T(8,128)} %cr.3) | copy-start | bytes 1572868
  2.7 30.4 %copy-start.4 = (s32[2,8,16]{2,1,0:T(8,128)S(1)}, s32[2,8,16]{2,1,0:T(8,128)}, u32[]{:S(2)}) copy-start(s32[2,8,16]{2,1,0:T(8,128)} %codes.1) | copy-start | bytes 3076
  2.7 16.6 %collective-permute-start = (f32[32,2048]{1,0:T(8,128)S(1)}, f32[32,2048]{1,0:T(8,128)S(1)}, u32[]{:S(2)}, u32[]{:S(2)}) collective-permute-start(f32[32,2048]{1,0:T(8,128)S(1)} %get-tuple-element.27), channel_id=1, source_target_pairs={{0,1},{1,2},{2,3},{3,4},{4,5},{5,6},{6,7},{7,8},{8,9},{9,10},{10,1... | collective-permute-start | bytes 786440 | tf_op jit(solution)/shard_map/ppermute | solution.py:530
  6.8 13.4 %collective-permute-start.1 = (f32[32,2048]{1,0:T(8,128)S(1)}, f32[32,2048]{1,0:T(8,128)S(1)}, u32[]{:S(2)}, u32[]{:S(2)}) collective-permute-start(f32[32,2048]{1,0:T(8,128)S(1)} %get-tuple-element.28), channel_id=1, source_target_pairs={{1,0},{2,1},{3,2},{4,3},{5,4},{6,5},{7,6},{8,7},{9,8},{10,9},{11,1... | collective-permute-start | bytes 786440 | tf_op jit(solution)/shard_map/ppermute | solution.py:530
  20.3 26.2 %collective-permute-start.3 = (f32[160,2048]{1,0:T(8,128)S(1)}, f32[160,2048]{1,0:T(8,128)S(1)}, u32[]{:S(2)}, u32[]{:S(2)}) collective-permute-start(f32[160,2048]{1,0:T(8,128)S(1)} %get-tuple-element.33), channel_id=1, source_target_pairs={{0,16},{1,17},{2,18},{3,19},{4,20},{5,21},{6,22},{7,23},{8,24},{9,... | collective-permute-start | bytes 3932168 | tf_op jit(solution)/shard_map/ppermute | solution.py:530
  23.9 22.5 %collective-permute-start.2 = (f32[136,2048]{1,0:T(8,128)S(1)}, f32[136,2048]{1,0:T(8,128)S(1)}, u32[]{:S(2)}, u32[]{:S(2)}) collective-permute-start(f32[136,2048]{1,0:T(8,128)S(1)} %get-tuple-element.32), channel_id=1, source_target_pairs={{16,32},{17,33},{18,34},{19,35},{20,36},{21,37},{22,38},{23,39},{2... | collective-permute-start | bytes 3342344 | tf_op jit(solution)/shard_map/ppermute | solution.py:530
  27.0 19.4 %collective-permute-start.4 = (f32[24,2048]{1,0:T(8,128)S(1)}, f32[24,2048]{1,0:T(8,128)S(1)}, u32[]{:S(2)}, u32[]{:S(2)}) collective-permute-start(f32[24,2048]{1,0:T(8,128)S(1)} %get-tuple-element.34), channel_id=1, source_target_pairs={{16,32},{17,33},{18,34},{19,35},{20,36},{21,37},{22,38},{23,39},{2... | collective-permute-start | bytes 589832 | tf_op jit(solution)/shard_map/ppermute | solution.py:530

commit v6 on v5

--- a/solution.py
+++ b/solution.py
@@ -263,7 +263,7 @@
     )(*(pltpu.with_memory_space_constraint(a, pltpu.HBM) for a in (inc, prec, cr, cc, codes)))
 
 
-def corner_body(pass_1, pass_2, bulk_in, up, dn, cor_o, bulk_e):
+def corner_body(up, dn, bulk_in, cor_o, bulk_e):
     del bulk_in
     cor_e = bulk_e.at[136:160]
     even = parity() == 0
@@ -280,18 +280,16 @@
         dst[16:24, :] = jnp.where(row < 4, up[16:24, :], dn[16:24, :])
 
     def both(from_up, from_dn, fwd, bwd):
-        up[...] = from_up[...]
-        dn[...] = from_dn[...]
         forward(from_up, from_dn, fwd)
         backward(from_up, from_dn, bwd)
 
     @pl.when(even)
     def _():
-        both(pass_1, pass_2, cor_e, cor_o)
+        both(up, dn, cor_e, cor_o)
 
     @pl.when(jnp.logical_not(even))
     def _():
-        both(pass_1, pass_2, cor_o, cor_e)
+        both(up, dn, cor_o, cor_e)
 
 
 def corner(pass_1, pass_2, bulk_e):
@@ -300,9 +298,9 @@
     return pl.pallas_call(
         corner_body,
         in_specs=[vmem] * 2 + [pl.BlockSpec(memory_space=pl.ANY)],
-        out_specs=[vmem] * 4,
-        out_shape=[f32(32, 2048), f32(32, 2048), f32(24, 2048), f32(160, 2048)],
-        input_output_aliases={2: 3},
+        out_specs=[vmem] * 2,
+        out_shape=[f32(24, 2048), f32(160, 2048)],
+        input_output_aliases={2: 1},
         compiler_params=pltpu.CompilerParams(vmem_limit_bytes=8 << 20),
         name="corner",
     )(pass_1, pass_2, bulk_e)
@@ -551,7 +549,8 @@
     bulk_o = permute(bulk_o, off_chip)
     pass_1 = permute(pass_1, up_on_even)
     pass_2 = permute(pass_2, down_on_even)
-    up, dn, cor_o, bulk_e = corner(pass_1, pass_2, bulk_e)
+    up, dn = pass_1, pass_2
+    cor_o, bulk_e = corner(up, dn, bulk_e)
     cor_o = permute(cor_o, off_chip)
     bulk_e = permute(bulk_e, on_chip)
     inc0, inc1, cr, cc, p0, p1, c0, c1 = prepare(inc, prec, cr, cc, codes)

time: 52.2 us -> 52.2 us (level)
  no operation moved by 1% of the time
where the time goes in v6:
time: 52.2 us; the launch traced here: 52 us
  starting transfers between devices  25.5 us (49%)
  waiting for transfers between devices  14.4 us (28%)
  Pallas kernels  11.4 us (22%)
  between operations  0.78 us (1%)
    ppermute x5, starting transfers between devices, permute(): return lax.ppermute(x, axes, pairs)  25.5 us
    ppermute x5, waiting for transfers between devices, permute(): return lax.ppermute(x, axes, pairs)  14.4 us
    pallas_call x1, Pallas kernels, first_steps(): pl.pallas_call(first_body, in_specs=[ON_VMEM] * 13 + [ON_HBM], out_specs=...  5.61 us
    pallas_call x1, Pallas kernels, last_step(): pl.pallas_call(last_body, in_specs=[ON_VMEM] * 8, out_specs=[ON_HBM] + [O...  3.21 us
    pallas_call x1, Pallas kernels, pack(): pl.pallas_call(pack_body, in_specs=[any_spec] * 5, out_specs=[vmem] * 4,...  1.98 us
  transfers between devices with their start and end apart: 5, of which 3 were waited for; matrix products, arithmetic and copies ran while one was open for 0% of the time, Pallas kernels for 7%

profile of v6, /device:TPU:59, one launch (start us, length us, event | category | flops | bytes accessed | tf_op | source)
XLA Modules:
  0.0 52.0 jit_solution(5873908556834641505)
XLA Ops:
  0.6 0.0 copy-start.1
  0.6 0.0 copy-start.3
  0.6 2.0 %pack.1 = (f32[136,2048]{1,0:T(8,128)S(1)}, f32[160,2048]{1,0:T(8,128)S(1)}, f32[32,2048]{1,0:T(8,128)S(1)}, f32[32,2048]{1,0:T(8,128)S(1)}) custom-call(f32[2,64,2048]{2,1,0:T(8,128)} %inc.3, f32[2,64,2048]{2,1,0:T(8,128)} %prec.3, f32[64,2048]{1,0:T(8,128)} %cr.3, f32[64,2048]{1,0:T(8,128)} %cc.3, s32[2,8,16]{2,1,0:T(8,128)} %codes.1), custom_call_target="tpu_custom_call" | custom-call | tf_op jit(solution)/shard_map/pack/pallas_call | solution.py:250
  2.6 0.0 copy-start
  2.7 0.0 copy-start.2
  2.7 0.0 copy-start.4
  2.7 4.1 %collective-permute-start = (f32[32,2048]{1,0:T(8,128)S(1)}, f32[32,2048]{1,0:T(8,128)S(1)}, u32[]{:S(2)}, u32[]{:S(2)}) collective-permute-start(f32[32,2048]{1,0:T(8,128)S(1)} %get-tuple-element.25), channel_id=1, source_target_pairs={{0,1},{1,2},{2,3},{3,4},{4,5},{5,6},{6,7},{7,8},{8,9},{9,10},{10,1... | collective-permute-start | bytes 786440 | tf_op jit(solution)/shard_map/ppermute | solution.py:528
  6.8 8.6 %collective-permute-start.1 = (f32[32,2048]{1,0:T(8,128)S(1)}, f32[32,2048]{1,0:T(8,128)S(1)}, u32[]{:S(2)}, u32[]{:S(2)}) collective-permute-start(f32[32,2048]{1,0:T(8,128)S(1)} %get-tuple-element.26), channel_id=1, source_target_pairs={{1,0},{2,1},{3,2},{4,3},{5,4},{6,5},{7,6},{8,7},{9,8},{10,9},{11,1... | collective-permute-start | bytes 786440 | tf_op jit(solution)/shard_map/ppermute | solution.py:528
  15.4 3.9 %collective-permute-done.up = f32[32,2048]{1,0:T(8,128)S(1)} collective-permute-done((f32[32,2048]{1,0:T(8,128)S(1)}, f32[32,2048]{1,0:T(8,128)S(1)}, u32[]{:S(2)}, u32[]{:S(2)}) %collective-permute-start) | collective-permute-done | bytes 262176 | tf_op jit(solution)/shard_map/ppermute | solution.py:528
  19.3 0.9 %collective-permute-done.1.dn = f32[32,2048]{1,0:T(8,128)S(1)} collective-permute-done((f32[32,2048]{1,0:T(8,128)S(1)}, f32[32,2048]{1,0:T(8,128)S(1)}, u32[]{:S(2)}, u32[]{:S(2)}) %collective-permute-start.1) | collective-permute-done | bytes 262176 | tf_op jit(solution)/shard_map/ppermute | solution.py:528
  20.2 3.6 %collective-permute-start.3 = (f32[160,2048]{1,0:T(8,128)S(1)}, f32[160,2048]{1,0:T(8,128)S(1)}, u32[]{:S(2)}, u32[]{:S(2)}) collective-permute-start(f32[160,2048]{1,0:T(8,128)S(1)} %get-tuple-element.29), channel_id=1, source_target_pairs={{0,16},{1,17},{2,18},{3,19},{4,20},{5,21},{6,22},{7,23},{8,24},{9,... | collective-permute-start | bytes 3932168 | tf_op jit(solution)/shard_map/ppermute | solution.py:528
  23.8 3.1 %collective-permute-start.2 = (f32[136,2048]{1,0:T(8,128)S(1)}, f32[136,2048]{1,0:T(8,128)S(1)}, u32[]{:S(2)}, u32[]{:S(2)}) collective-permute-start(f32[136,2048]{1,0:T(8,128)S(1)} %get-tuple-element.27), channel_id=1, source_target_pairs={{16,32},{17,33},{18,34},{19,35},{20,36},{21,37},{22,38},{23,39},{2... | collective-permute-start | bytes 3342344 | tf_op jit(solution)/shard_map/ppermute | solution.py:528
  27.0 6.0 %collective-permute-start.4 = (f32[24,2048]{1,0:T(8,128)S(1)}, f32[24,2048]{1,0:T(8,128)S(1)}, u32[]{:S(2)}, u32[]{:S(2)}) collective-permute-start(f32[24,2048]{1,0:T(8,128)S(1)} %get-tuple-element.30), channel_id=1, source_target_pairs={{16,32},{17,33},{18,34},{19,35},{20,36},{21,37},{22,38},{23,39},{2... | collective-permute-start | bytes 589832 | tf_op jit(solution)/shard_map/ppermute | solution.py:528
  33.0 0.0 copy-done.1
  33.0 0.0 copy-done.3
  33.0 0.0 copy-done
  33.1 0.0 copy-done.2
  33.1 0.0 copy-done.4
  33.1 0.5 %prepare.1 = (f32[16,80,128]{2,1,0:T(8,128)S(1)}, f32[16,80,128]{2,1,0:T(8,128)S(1)}, f32[16,80,128]{2,1,0:T(8,128)S(1)}, f32[16,80,128]{2,1,0:T(8,128)S(1)}, f3...) custom-call(f32[2,64,2048]{2,1,0:T(8,128)S(1)} %copy-done, ...), custom_call_target="tpu_custom_call" | custom-call | tf_op jit(solution)/shard_map/prepare/pallas_call | solution.py:483
  33.6 3.2 %last.1 = (f32[2,64,2048]{2,1,0:T(8,128)}, f32[10,16,8,128]{3,2,1,0:T(8,128)S(1)}, f32[10,16,8,128]{3,2,1,0:T(8,128)S(1)}, f32[16,80,128]{2,1,0:T(8,128)S(1)}, f...) custom-call(f32[32,2048]{1,0:T(8,128)S(1)} %collective-permute-done., ...), custom_call_target="tpu_custom_call", output_to_operand_aliasing={{3}: (2, {}), {4}: (3, {}), {5}: (4, {}), {6}: (5, {}), {7}... | custom-call | tf_op jit(solution)/shard_map/last/pallas_call | solution.py:494
  36.8 9.5 %collective-permute-done.4.cor_o = f32[24,2048]{1,0:T(8,128)S(1)} collective-permute-done((f32[24,2048]{1,0:T(8,128)S(1)}, f32[24,2048]{1,0:T(8,128)S(1)}, u32[]{:S(2)}, u32[]{:S(2)}) %collective-permute-start.4) | collective-permute-done | bytes 196640 | tf_op jit(solution)/shard_map/ppermute | solution.py:528
  46.4 0.0 collective-permute-done.2.bulk_o
  46.4 0.0 collective-permute-done.3.bulk_e
  46.4 5.6 %first.1 = (f32[2,64,2048]{2,1,0:T(8,128)}, f32[2,64,2048]{2,1,0:T(8,128)}, f32[16,80,128]{2,1,0:T(8,128)S(1)}, f32[16,80,128]{2,1,0:T(8,128)S(1)}) custom-call(f32[32,2048]{1,0:T(8,128)S(1)} %collective-permute-done.up, f32[32,2048]{1,0:T(8,128)S(1)} %collective-permute-done.1.dn, ...), custom_call_target="tpu_custom_call", output_to_operand_aliasing={{0}: (13, {}), {2}: (11, {}), {3}: (12, {})} | custom-call | tf_op jit(solution)/shard_map/first/pallas_call | solution.py:507
  (1 shorter events, 0.0 us)
Async XLA Ops:
  0.6 32.4 %copy-start.1 = (f32[2,64,2048]{2,1,0:T(8,128)S(1)}, f32[2,64,2048]{2,1,0:T(8,128)}, u32[]{:S(2)}) copy-start(f32[2,64,2048]{2,1,0:T(8,128)} %prec.3) | copy-start | bytes 3145732
  0.6 32.4 %copy-start.3 = (f32[64,2048]{1,0:T(8,128)S(1)}, f32[64,2048]{1,0:T(8,128)}, u32[]{:S(2)}) copy-start(f32[64,2048]{1,0:T(8,128)} %cc.3) | copy-start | bytes 1572868
  2.6 30.4 %copy-start = (f32[2,64,2048]{2,1,0:T(8,128)S(1)}, f32[2,64,2048]{2,1,0:T(8,128)}, u32[]{:S(2)}) copy-start(f32[2,64,2048]{2,1,0:T(8,128)} %inc.3) | copy-start | bytes 3145732
  2.7 30.4 %copy-start.2 = (f32[64,2048]{1,0:T(8,128)S(1)}, f32[64,2048]{1,0:T(8,128)}, u32[]{:S(2)}) copy-start(f32[64,2048]{1,0:T(8,128)} %cr.3) | copy-start | bytes 1572868
  2.7 30.4 %copy-start.4 = (s32[2,8,16]{2,1,0:T(8,128)S(1)}, s32[2,8,16]{2,1,0:T(8,128)}, u32[]{:S(2)}) copy-start(s32[2,8,16]{2,1,0:T(8,128)} %codes.1) | copy-start | bytes 3076
  2.7 16.6 %collective-permute-start = (f32[32,2048]{1,0:T(8,128)S(1)}, f32[32,2048]{1,0:T(8,128)S(1)}, u32[]{:S(2)}, u32[]{:S(2)}) collective-permute-start(f32[32,2048]{1,0:T(8,128)S(1)} %get-tuple-element.25), channel_id=1, source_target_pairs={{0,1},{1,2},{2,3},{3,4},{4,5},{5,6},{6,7},{7,8},{8,9},{9,10},{10,1... | collective-permute-start | bytes 786440 | tf_op jit(solution)/shard_map/ppermute | solution.py:528
  6.8 13.4 %collective-permute-start.1 = (f32[32,2048]{1,0:T(8,128)S(1)}, f32[32,2048]{1,0:T(8,128)S(1)}, u32[]{:S(2)}, u32[]{:S(2)}) collective-permute-start(f32[32,2048]{1,0:T(8,128)S(1)} %get-tuple-element.26), channel_id=1, source_target_pairs={{1,0},{2,1},{3,2},{4,3},{5,4},{6,5},{7,6},{8,7},{9,8},{10,9},{11,1... | collective-permute-start | bytes 786440 | tf_op jit(solution)/shard_map/ppermute | solution.py:528
  20.2 26.2 %collective-permute-start.3 = (f32[160,2048]{1,0:T(8,128)S(1)}, f32[160,2048]{1,0:T(8,128)S(1)}, u32[]{:S(2)}, u32[]{:S(2)}) collective-permute-start(f32[160,2048]{1,0:T(8,128)S(1)} %get-tuple-element.29), channel_id=1, source_target_pairs={{0,16},{1,17},{2,18},{3,19},{4,20},{5,21},{6,22},{7,23},{8,24},{9,... | collective-permute-start | bytes 3932168 | tf_op jit(solution)/shard_map/ppermute | solution.py:528
  23.8 22.5 %collective-permute-start.2 = (f32[136,2048]{1,0:T(8,128)S(1)}, f32[136,2048]{1,0:T(8,128)S(1)}, u32[]{:S(2)}, u32[]{:S(2)}) collective-permute-start(f32[136,2048]{1,0:T(8,128)S(1)} %get-tuple-element.27), channel_id=1, source_target_pairs={{16,32},{17,33},{18,34},{19,35},{20,36},{21,37},{22,38},{23,39},{2... | collective-permute-start | bytes 3342344 | tf_op jit(solution)/shard_map/ppermute | solution.py:528
  27.0 19.4 %collective-permute-start.4 = (f32[24,2048]{1,0:T(8,128)S(1)}, f32[24,2048]{1,0:T(8,128)S(1)}, u32[]{:S(2)}, u32[]{:S(2)}) collective-permute-start(f32[24,2048]{1,0:T(8,128)S(1)} %get-tuple-element.30), channel_id=1, source_target_pairs={{16,32},{17,33},{18,34},{19,35},{20,36},{21,37},{22,38},{23,39},{2... | collective-permute-start | bytes 589832 | tf_op jit(solution)/shard_map/ppermute | solution.py:528
